TPU v7x, 32 devices: a whole 2x2x4 slice. The times are simulated.
32 devices in a mesh: gz: 16 (over z, y, core), gy: 2 (over x).
Axes of the slice: x: 2, y: 2, z: 4, core: 2. Of those that a mesh axis runs over, the one named last changes fastest.
Arguments:
- estimate: float32 [256, 64, 512], P('gz', 'gy'), may hold values from 0.5 to 2
- measured: float32 [4, 256, 64, 512], P(None, 'gz', 'gy'), may hold values from 0.25 to 4
- psf_z: float32 [4, 31], replicated, may hold values from 0.1 to 1
- psf_y: float32 [4, 15], replicated, may hold values from 0.1 to 1
- psf_x: float32 [4, 15], replicated, may hold values from 0.1 to 1
- extents: int32 [4, 3], replicated, may hold values from 9 to 31, as said below
- order: int32 [4], replicated, may hold values from 0 to 3, each once
Outputs:
- updated: float32 [256, 64, 512], P('gz', 'gy')
Inputs may be any that keep to these rules, and one draw needn't show every extreme that they name: `extents`: every extent is odd; along z it lies in 9 to 31, along y and x in 9 to 15; in every draw some view has extent 31 along z and some view has extent 15 along y.
All inputs are finite; a program needn't handle non-finite values.
Results may differ from a plain program's by a relative error of at most 0.0001.
Values sent between devices are 32-bit elements; how exact they have to be, the bound alone decides.
A program may use at most 64 MiB of HBM per device.

v0:
```python
import jax
import jax.numpy as jnp
from jax import lax
from jax.sharding import PartitionSpec as P


def with_halo(value, sides, width):
    for axis, dim in sides:
        size, length = (lax.axis_size(axis), value.shape[dim])
        up = [(i, (i + 1) % size) for i in range(size - 1)]
        down = [(j, i) for i, j in up]
        last = lax.slice_in_dim(value, length - width, length, axis=dim)
        initial = lax.slice_in_dim(value, 0, width, axis=dim)
        before = lax.ppermute(last, axis, up)
        after = lax.ppermute(initial, axis, down)
        value = jnp.concatenate([before, value, after], axis=dim)
    return value


def line_taps(profile, reach_cells, tap_reach):
    offsets = jnp.arange(2 * tap_reach + 1, dtype=jnp.int32) - tap_reach
    kept = jnp.where(jnp.abs(offsets) <= reach_cells, profile, jnp.zeros_like(profile))
    return kept / jnp.sum(kept)


def correlate_padded(padded, weights, along_axis, tap_reach, length, flipped):
    total = None
    for offset in range(2 * tap_reach + 1):
        start = 2 * tap_reach - offset if flipped else offset
        piece = lax.slice_in_dim(padded, start, start + length, axis=along_axis)
        term = weights[offset] * piece
        total = term if total is None else total + term
    return total


def blur(field, weights_z, weights_y, weights_x, flipped):
    planes = field.shape[0]
    rows = field.shape[1]
    padded = with_halo(field, (("gz", 0),), 15)
    result = correlate_padded(padded, weights_z, 0, 15, planes, flipped)
    widened = with_halo(result, (("gy", 1),), 7)
    result = correlate_padded(widened, weights_y, 1, 7, rows, flipped)
    result = jnp.pad(result, ((0, 0), (0, 0), (7, 7)))
    return correlate_padded(result, weights_x, 2, 7, field.shape[2], flipped)


def on_device(estimate, measured, psf_z, psf_y, psf_x, extents, order):
    current = estimate
    for position in range(measured.shape[0]):
        view = order[position]
        radii = (extents[view] - 1) // 2
        weights_z = line_taps(psf_z[view], radii[0], 15)
        weights_y = line_taps(psf_y[view], radii[1], 7)
        weights_x = line_taps(psf_x[view], radii[2], 7)
        recorded = lax.dynamic_index_in_dim(measured, view, 0, keepdims=False)
        blurred = blur(current, weights_z, weights_y, weights_x, False)
        ratio = recorded / blurred
        current = current * blur(ratio, weights_z, weights_y, weights_x, True)
    return current


def solution(mesh):
    return jax.shard_map(
        on_device,
        mesh=mesh,
        in_specs=(P("gz", "gy", None), P(None, "gz", "gy", None), P(), P(), P(), P(), P()),
        out_specs=P("gz", "gy", None),
        check_vma=False,
    )
```

profile of v0, /device:TPU:20, one launch (start us, length us, event | category | flops | bytes accessed | tf_op | source)
XLA Modules:
  0.0 693.5 jit_solution(1750508661390420618)
XLA Ops:
  19.6 5.7 fusion.1218
  32.3 23.4 %fusion.1168 = f32[16,32,512]{2,1,0:T(8,128)S(1)} fusion(f32[31,32,512]{2,1,0:T(8,128)S(1)} %constant_dynamic-update-slice_fusion.2, f32[31,32,512]{2,1,0:T(8,128)S(1)} %get-tuple-element.59, f32[16,32,512]{2,1,0:T(8,128)S(1)} %copy-done, f32[]{:T(128)} %bitcast.41, f32[]{:T(128)} %bitcast.40, f32[]{:T(128)} %bitcast.39, f32[]{:T(128)} %bitcast.38, ...), kind=kLoop, calls=%fused_computation.1895 | loop fusion | flops 15990784 | bytes 33554556 | tf_op jit(solution)/shard_map/add | solution.py:32
  57.1 4.6 collective-permute-start.2
  67.0 11.8 %fusion.269 = f32[16,32,512]{2,1,0:T(8,128)S(1)} fusion(f32[16,32,512]{2,1,0:T(8,128)S(1)} %fusion.1168, f32[16,7,512]{2,1,0:T(8,128)S(1)} %collective-permute-done.3, f32[16,7,512]{2,1,0:T(8,128)S(1)} %collective-permute-done.2, f32[]{:T(128)} %bitcast.55, f32[]{:T(128)} %bitcast.54, f32[]{:T(128)} %bitcast.53, f32[]{:T(128)} %bitcast.52, f32[]{:T(128)} %bitcast.51, ...), kind=kLoop, calls=%fused_computation.965 | loop fusion | flops 11272192 | bytes 2555964 | tf_op jit(solution)/shard_map/add | solution.py:32
  78.8 14.4 %fusion.319 = f32[16,32,512]{2,1,0:T(8,128)S(1)} fusion(f32[16,32,512]{2,1,0:T(8,128)S(1)} %fusion.269, f32[4,16,32,512]{3,2,1,0:T(8,128)} %param.8, s32[]{:T(128)S(6)} %select_n.81, f32[]{:T(128)} %bitcast.69, f32[]{:T(128)} %bitcast.68, f32[]{:T(128)} %bitcast.67, f32[]{:T(128)} %bitcast.66, f32[]{:T(128)} %bitcast.65, f32[]{:T(128)} %bitcast.64, ...), kind=kLoop, calls=%fused_computation.1015 | loop fusion | flops 7864320 | bytes 3145792 | tf_op jit(solution)/shard_map/div | solution.py:57
  95.3 3.6 collective-permute-start.4
  99.0 20.4 %collective-permute-done.5 = f32[15,32,512]{2,1,0:T(8,128)S(1)} collective-permute-done((f32[15,32,512]{2,1,0:T(8,128)S(1)}, f32[15,32,512]{2,1,0:T(8,128)S(1)}, u32[]{:S(2)}, u32[]{:S(2)}) %collective-permute-start.5) | collective-permute-done | bytes 983072 | tf_op jit(solution)/shard_map/ppermute | solution.py:14
  119.3 23.4 %fusion.1055 = f32[16,32,512]{2,1,0:T(8,128)S(1)} fusion(f32[16,32,512]{2,1,0:T(8,128)S(1)} %fusion.319, f32[15,32,512]{2,1,0:T(8,128)S(1)} %collective-permute-done.5, f32[15,32,512]{2,1,0:T(8,128)S(1)} %collective-permute-done.4, f32[]{:T(128)} %bitcast.41, f32[]{:T(128)} %bitcast.40, f32[]{:T(128)} %bitcast.39, f32[]{:T(128)} %bitcast.38, f32[]{:T(128)} %bitcast.37, ...), kind=kLoop, calls=%fused_computation.1751 | loop fusion | flops 23855104 | bytes 4063356 | tf_op jit(solution)/shard_map/add | solution.py:32
  142.8 4.4 collective-permute-start.7
  151.1 4.4 collective-permute-done.6
  155.5 11.8 %fusion.231 = f32[16,32,512]{2,1,0:T(8,128)S(1)} fusion(f32[16,32,512]{2,1,0:T(8,128)S(1)} %fusion.1055, f32[16,7,512]{2,1,0:T(8,128)S(1)} %collective-permute-done.7, f32[16,7,512]{2,1,0:T(8,128)S(1)} %collective-permute-done.6, f32[]{:T(128)} %bitcast.55, f32[]{:T(128)} %bitcast.54, f32[]{:T(128)} %bitcast.53, f32[]{:T(128)} %bitcast.52, f32[]{:T(128)} %bitcast.51, ...), kind=kLoop, calls=%fused_computation.927 | loop fusion | flops 11272192 | bytes 2555964 | tf_op jit(solution)/shard_map/add | solution.py:32
  167.3 13.3 %fusion.348 = f32[16,32,512]{2,1,0:T(8,128)S(1)} fusion(f32[16,32,512]{2,1,0:T(8,128)S(1)} %copy-done, f32[16,32,512]{2,1,0:T(8,128)S(1)} %fusion.231, f32[]{:T(128)} %bitcast.69, f32[]{:T(128)} %bitcast.68, f32[]{:T(128)} %bitcast.67, f32[]{:T(128)} %bitcast.66, f32[]{:T(128)} %bitcast.65, f32[]{:T(128)} %bitcast.64, f32[]{:T(128)} %bitcast.63, ...), kind=kLoop, calls=%fused_computation.1044 | loop fusion | flops 7864320 | bytes 3145788 | tf_op jit(solution)/shard_map/mul | solution.py:58
  187.4 17.6 %collective-permute-done.9 = f32[15,32,512]{2,1,0:T(8,128)S(1)} collective-permute-done((f32[15,32,512]{2,1,0:T(8,128)S(1)}, f32[15,32,512]{2,1,0:T(8,128)S(1)}, u32[]{:S(2)}, u32[]{:S(2)}) %collective-permute-start.9) | collective-permute-done | bytes 983072 | tf_op jit(solution)/shard_map/ppermute | solution.py:15
  204.9 23.5 %fusion.969 = f32[16,32,512]{2,1,0:T(8,128)S(1)} fusion(f32[16,32,512]{2,1,0:T(8,128)S(1)} %fusion.348, f32[15,32,512]{2,1,0:T(8,128)S(1)} %collective-permute-done.9, f32[15,32,512]{2,1,0:T(8,128)S(1)} %collective-permute-done.8, f32[]{:T(128)} %bitcast.111, f32[]{:T(128)} %bitcast.110, f32[]{:T(128)} %bitcast.109, f32[]{:T(128)} %bitcast.108, ...), kind=kLoop, calls=%fused_computation.1665 | loop fusion | flops 23855104 | bytes 4063356 | tf_op jit(solution)/shard_map/add | solution.py:32
  229.8 4.6 collective-permute-start.10
  238.2 11.9 %fusion.193 = f32[16,32,512]{2,1,0:T(8,128)S(1)} fusion(f32[16,32,512]{2,1,0:T(8,128)S(1)} %fusion.969, f32[16,7,512]{2,1,0:T(8,128)S(1)} %collective-permute-done.11, f32[16,7,512]{2,1,0:T(8,128)S(1)} %collective-permute-done.10, f32[]{:T(128)} %bitcast.125, f32[]{:T(128)} %bitcast.124, f32[]{:T(128)} %bitcast.123, f32[]{:T(128)} %bitcast.122, ...), kind=kLoop, calls=%fused_computation.889 | loop fusion | flops 11272192 | bytes 2555964 | tf_op jit(solution)/shard_map/add | solution.py:32
  250.1 14.3 %fusion.377 = f32[16,32,512]{2,1,0:T(8,128)S(1)} fusion(f32[16,32,512]{2,1,0:T(8,128)S(1)} %fusion.193, f32[4,16,32,512]{3,2,1,0:T(8,128)} %param.8, s32[]{:T(128)S(6)} %select_n.86, f32[]{:T(128)} %bitcast.139, f32[]{:T(128)} %bitcast.138, f32[]{:T(128)} %bitcast.137, f32[]{:T(128)} %bitcast.136, f32[]{:T(128)} %bitcast.135, f32[]{:T(128)} %bitcast.134, ...), kind=kLoop, calls=%fused_computation.1073 | loop fusion | flops 7864320 | bytes 3145792 | tf_op jit(solution)/shard_map/div | solution.py:57
  266.6 3.6 collective-permute-start.12
  270.2 20.4 %collective-permute-done.13 = f32[15,32,512]{2,1,0:T(8,128)S(1)} collective-permute-done((f32[15,32,512]{2,1,0:T(8,128)S(1)}, f32[15,32,512]{2,1,0:T(8,128)S(1)}, u32[]{:S(2)}, u32[]{:S(2)}) %collective-permute-start.13) | collective-permute-done | bytes 983072 | tf_op jit(solution)/shard_map/ppermute | solution.py:14
  290.6 23.5 %fusion.883 = f32[16,32,512]{2,1,0:T(8,128)S(1)} fusion(f32[16,32,512]{2,1,0:T(8,128)S(1)} %fusion.377, f32[15,32,512]{2,1,0:T(8,128)S(1)} %collective-permute-done.13, f32[15,32,512]{2,1,0:T(8,128)S(1)} %collective-permute-done.12, f32[]{:T(128)} %bitcast.111, f32[]{:T(128)} %bitcast.110, f32[]{:T(128)} %bitcast.109, f32[]{:T(128)} %bitcast.108, ...), kind=kLoop, calls=%fused_computation.1579 | loop fusion | flops 23855104 | bytes 4063356 | tf_op jit(solution)/shard_map/add | solution.py:32
  314.2 4.4 collective-permute-start.15
  322.4 4.4 collective-permute-done.14
  326.8 11.9 %fusion.155 = f32[16,32,512]{2,1,0:T(8,128)S(1)} fusion(f32[16,32,512]{2,1,0:T(8,128)S(1)} %fusion.883, f32[16,7,512]{2,1,0:T(8,128)S(1)} %collective-permute-done.15, f32[16,7,512]{2,1,0:T(8,128)S(1)} %collective-permute-done.14, f32[]{:T(128)} %bitcast.125, f32[]{:T(128)} %bitcast.124, f32[]{:T(128)} %bitcast.123, f32[]{:T(128)} %bitcast.122, ...), kind=kLoop, calls=%fused_computation.851 | loop fusion | flops 11272192 | bytes 2555964 | tf_op jit(solution)/shard_map/add | solution.py:32
  338.7 13.2 %fusion.406 = f32[16,32,512]{2,1,0:T(8,128)S(1)} fusion(f32[16,32,512]{2,1,0:T(8,128)S(1)} %fusion.348, f32[16,32,512]{2,1,0:T(8,128)S(1)} %fusion.155, f32[]{:T(128)} %bitcast.139, f32[]{:T(128)} %bitcast.138, f32[]{:T(128)} %bitcast.137, f32[]{:T(128)} %bitcast.136, f32[]{:T(128)} %bitcast.135, f32[]{:T(128)} %bitcast.134, f32[]{:T(128)} %bitcast.133, ...), kind=kLoop, calls=%fused_computation.1102 | loop fusion | flops 7864320 | bytes 3145788 | tf_op jit(solution)/shard_map/mul | solution.py:58
  359.8 16.4 %collective-permute-done.17 = f32[15,32,512]{2,1,0:T(8,128)S(1)} collective-permute-done((f32[15,32,512]{2,1,0:T(8,128)S(1)}, f32[15,32,512]{2,1,0:T(8,128)S(1)}, u32[]{:S(2)}, u32[]{:S(2)}) %collective-permute-start.17) | collective-permute-done | bytes 983072 | tf_op jit(solution)/shard_map/ppermute | solution.py:15
  376.2 23.5 %fusion.797 = f32[16,32,512]{2,1,0:T(8,128)S(1)} fusion(f32[16,32,512]{2,1,0:T(8,128)S(1)} %fusion.406, f32[15,32,512]{2,1,0:T(8,128)S(1)} %collective-permute-done.17, f32[15,32,512]{2,1,0:T(8,128)S(1)} %collective-permute-done.16, f32[]{:T(128)} %bitcast.181, f32[]{:T(128)} %bitcast.180, f32[]{:T(128)} %bitcast.179, f32[]{:T(128)} %bitcast.178, ...), kind=kLoop, calls=%fused_computation.1493 | loop fusion | flops 23855104 | bytes 4063356 | tf_op jit(solution)/shard_map/add | solution.py:32
  401.1 4.6 collective-permute-start.18
  409.5 11.9 %fusion.117 = f32[16,32,512]{2,1,0:T(8,128)S(1)} fusion(f32[16,32,512]{2,1,0:T(8,128)S(1)} %fusion.797, f32[16,7,512]{2,1,0:T(8,128)S(1)} %collective-permute-done.19, f32[16,7,512]{2,1,0:T(8,128)S(1)} %collective-permute-done.18, f32[]{:T(128)} %bitcast.195, f32[]{:T(128)} %bitcast.194, f32[]{:T(128)} %bitcast.193, f32[]{:T(128)} %bitcast.192, ...), kind=kLoop, calls=%fused_computation.813 | loop fusion | flops 11272192 | bytes 2555964 | tf_op jit(solution)/shard_map/add | solution.py:32
  421.4 14.3 %fusion.435 = f32[16,32,512]{2,1,0:T(8,128)S(1)} fusion(f32[16,32,512]{2,1,0:T(8,128)S(1)} %fusion.117, f32[4,16,32,512]{3,2,1,0:T(8,128)} %param.8, s32[]{:T(128)S(6)} %select_n.91, f32[]{:T(128)} %bitcast.209, f32[]{:T(128)} %bitcast.208, f32[]{:T(128)} %bitcast.207, f32[]{:T(128)} %bitcast.206, f32[]{:T(128)} %bitcast.205, f32[]{:T(128)} %bitcast.204, ...), kind=kLoop, calls=%fused_computation.1131 | loop fusion | flops 7864320 | bytes 3145792 | tf_op jit(solution)/shard_map/div | solution.py:57
  437.8 3.6 collective-permute-start.20
  441.5 20.4 %collective-permute-done.21 = f32[15,32,512]{2,1,0:T(8,128)S(1)} collective-permute-done((f32[15,32,512]{2,1,0:T(8,128)S(1)}, f32[15,32,512]{2,1,0:T(8,128)S(1)}, u32[]{:S(2)}, u32[]{:S(2)}) %collective-permute-start.21) | collective-permute-done | bytes 983072 | tf_op jit(solution)/shard_map/ppermute | solution.py:14
  461.9 23.5 %fusion.711 = f32[16,32,512]{2,1,0:T(8,128)S(1)} fusion(f32[16,32,512]{2,1,0:T(8,128)S(1)} %fusion.435, f32[15,32,512]{2,1,0:T(8,128)S(1)} %collective-permute-done.21, f32[15,32,512]{2,1,0:T(8,128)S(1)} %collective-permute-done.20, f32[]{:T(128)} %bitcast.181, f32[]{:T(128)} %bitcast.180, f32[]{:T(128)} %bitcast.179, f32[]{:T(128)} %bitcast.178, ...), kind=kLoop, calls=%fused_computation.1407 | loop fusion | flops 23855104 | bytes 4063356 | tf_op jit(solution)/shard_map/add | solution.py:32
  485.4 4.4 collective-permute-start.23
  493.7 4.4 collective-permute-done.22
  498.1 11.9 %fusion.79 = f32[16,32,512]{2,1,0:T(8,128)S(1)} fusion(f32[16,32,512]{2,1,0:T(8,128)S(1)} %fusion.711, f32[16,7,512]{2,1,0:T(8,128)S(1)} %collective-permute-done.23, f32[16,7,512]{2,1,0:T(8,128)S(1)} %collective-permute-done.22, f32[]{:T(128)} %bitcast.195, f32[]{:T(128)} %bitcast.194, f32[]{:T(128)} %bitcast.193, f32[]{:T(128)} %bitcast.192, ...), kind=kLoop, calls=%fused_computation.775 | loop fusion | flops 11272192 | bytes 2555964 | tf_op jit(solution)/shard_map/add | solution.py:32
  510.0 13.2 %fusion.464 = f32[16,32,512]{2,1,0:T(8,128)S(1)} fusion(f32[16,32,512]{2,1,0:T(8,128)S(1)} %fusion.406, f32[16,32,512]{2,1,0:T(8,128)S(1)} %fusion.79, f32[]{:T(128)} %bitcast.209, f32[]{:T(128)} %bitcast.208, f32[]{:T(128)} %bitcast.207, f32[]{:T(128)} %bitcast.206, f32[]{:T(128)} %bitcast.205, f32[]{:T(128)} %bitcast.204, f32[]{:T(128)} %bitcast.203, ...), kind=kLoop, calls=%fused_computation.1160 | loop fusion | flops 7864320 | bytes 3145788 | tf_op jit(solution)/shard_map/mul | solution.py:58
  529.9 16.5 %collective-permute-done.25 = f32[15,32,512]{2,1,0:T(8,128)S(1)} collective-permute-done((f32[15,32,512]{2,1,0:T(8,128)S(1)}, f32[15,32,512]{2,1,0:T(8,128)S(1)}, u32[]{:S(2)}, u32[]{:S(2)}) %collective-permute-start.25) | collective-permute-done | bytes 983072 | tf_op jit(solution)/shard_map/ppermute | solution.py:15
  546.4 23.5 %fusion.625 = f32[16,32,512]{2,1,0:T(8,128)S(1)} fusion(f32[16,32,512]{2,1,0:T(8,128)S(1)} %fusion.464, f32[15,32,512]{2,1,0:T(8,128)S(1)} %collective-permute-done.25, f32[15,32,512]{2,1,0:T(8,128)S(1)} %collective-permute-done.24, f32[]{:T(128)} %bitcast.251, f32[]{:T(128)} %bitcast.250, f32[]{:T(128)} %bitcast.249, f32[]{:T(128)} %bitcast.248, ...), kind=kLoop, calls=%fused_computation.1321 | loop fusion | flops 23855104 | bytes 4063356 | tf_op jit(solution)/shard_map/add | solution.py:32
  571.2 4.6 collective-permute-start.26
  579.7 11.9 %fusion.41 = f32[16,32,512]{2,1,0:T(8,128)S(1)} fusion(f32[16,32,512]{2,1,0:T(8,128)S(1)} %fusion.625, f32[16,7,512]{2,1,0:T(8,128)S(1)} %collective-permute-done.27, f32[16,7,512]{2,1,0:T(8,128)S(1)} %collective-permute-done.26, f32[]{:T(128)} %bitcast.265, f32[]{:T(128)} %bitcast.264, f32[]{:T(128)} %bitcast.263, f32[]{:T(128)} %bitcast.262, ...), kind=kLoop, calls=%fused_computation.737 | loop fusion | flops 11272192 | bytes 2555964 | tf_op jit(solution)/shard_map/add | solution.py:32
  591.6 14.3 %fusion.493 = f32[16,32,512]{2,1,0:T(8,128)S(1)} fusion(f32[16,32,512]{2,1,0:T(8,128)S(1)} %fusion.41, f32[4,16,32,512]{3,2,1,0:T(8,128)} %param.8, s32[]{:T(128)S(6)} %select_n.96, f32[]{:T(128)} %bitcast.279, f32[]{:T(128)} %bitcast.278, f32[]{:T(128)} %bitcast.277, f32[]{:T(128)} %bitcast.276, f32[]{:T(128)} %bitcast.275, f32[]{:T(128)} %bitcast.274, ...), kind=kLoop, calls=%fused_computation.1189 | loop fusion | flops 7864320 | bytes 3145792 | tf_op jit(solution)/shard_map/div | solution.py:57
  608.0 3.6 collective-permute-start.28
  611.7 19.7 %collective-permute-done.29 = f32[15,32,512]{2,1,0:T(8,128)S(1)} collective-permute-done((f32[15,32,512]{2,1,0:T(8,128)S(1)}, f32[15,32,512]{2,1,0:T(8,128)S(1)}, u32[]{:S(2)}, u32[]{:S(2)}) %collective-permute-start.29) | collective-permute-done | bytes 983072 | tf_op jit(solution)/shard_map/ppermute | solution.py:14
  631.3 23.5 %fusion.539 = f32[16,32,512]{2,1,0:T(8,128)S(1)} fusion(f32[16,32,512]{2,1,0:T(8,128)S(1)} %fusion.493, f32[15,32,512]{2,1,0:T(8,128)S(1)} %collective-permute-done.29, f32[15,32,512]{2,1,0:T(8,128)S(1)} %collective-permute-done.28, f32[]{:T(128)} %bitcast.251, f32[]{:T(128)} %bitcast.250, f32[]{:T(128)} %bitcast.249, f32[]{:T(128)} %bitcast.248, ...), kind=kLoop, calls=%fused_computation.1235 | loop fusion | flops 23855104 | bytes 4063356 | tf_op jit(solution)/shard_map/add | solution.py:32
  654.9 4.2 collective-permute-start.31
  663.0 4.4 collective-permute-done.30
  667.4 11.9 %fusion.3 = f32[16,32,512]{2,1,0:T(8,128)S(1)} fusion(f32[16,32,512]{2,1,0:T(8,128)S(1)} %fusion.539, f32[16,7,512]{2,1,0:T(8,128)S(1)} %collective-permute-done.31, f32[16,7,512]{2,1,0:T(8,128)S(1)} %collective-permute-done.30, f32[]{:T(128)} %bitcast.265, f32[]{:T(128)} %bitcast.264, f32[]{:T(128)} %bitcast.263, f32[]{:T(128)} %bitcast.262, f32[]{:T(128)} %bitcast.261, ...), kind=kLoop, calls=%fused_computation.699 | loop fusion | flops 11272192 | bytes 2555964 | tf_op jit(solution)/shard_map/add | solution.py:32
  679.3 14.0 %fusion.522 = f32[16,32,512]{2,1,0:T(8,128)} fusion(f32[16,32,512]{2,1,0:T(8,128)S(1)} %fusion.464, f32[16,32,512]{2,1,0:T(8,128)S(1)} %fusion.3, f32[]{:T(128)} %bitcast.279, f32[]{:T(128)} %bitcast.278, f32[]{:T(128)} %bitcast.277, f32[]{:T(128)} %bitcast.276, f32[]{:T(128)} %bitcast.275, f32[]{:T(128)} %bitcast.274, f32[]{:T(128)} %bitcast.273, ...), kind=kLoop, calls=%fused_computation.1218 | loop fusion | flops 7864320 | bytes 3145788 | tf_op jit(solution)/shard_map/mul | solution.py:58
  (105 shorter events, 86.4 us)
Async XLA Ops:
  0.0 8.8 %copy-start.1 = (s32[4]{0:T(128)S(1)}, s32[4]{0:T(128)}, u32[]{:S(2)}) copy-start(s32[4]{0:T(128)} %param.13) | copy-start | bytes 52
  0.0 16.9 %copy-start.2 = (s32[4,3]{1,0:T(4,128)S(1)}, s32[4,3]{1,0:T(4,128)}, u32[]{:S(2)}) copy-start(s32[4,3]{1,0:T(4,128)} %param.12) | copy-start | bytes 148
  0.0 19.6 %copy-start.3 = (f32[4,15]{1,0:T(4,128)S(1)}, f32[4,15]{1,0:T(4,128)}, u32[]{:S(2)}) copy-start(f32[4,15]{1,0:T(4,128)} %param.11) | copy-start | bytes 724
  0.0 19.6 %copy-start.4 = (f32[4,15]{1,0:T(4,128)S(1)}, f32[4,15]{1,0:T(4,128)}, u32[]{:S(2)}) copy-start(f32[4,15]{1,0:T(4,128)} %param.10) | copy-start | bytes 724
  0.0 25.3 %copy-start.5 = (f32[4,31]{1,0:T(4,128)S(1)}, f32[4,31]{1,0:T(4,128)}, u32[]{:S(2)}) copy-start(f32[4,31]{1,0:T(4,128)} %param.9) | copy-start | bytes 1492
  3.1 28.9 %copy-start = (f32[16,32,512]{2,1,0:T(8,128)S(1)}, f32[16,32,512]{2,1,0:T(8,128)}, u32[]{:S(2)}) copy-start(f32[16,32,512]{2,1,0:T(8,128)} %param.7) | copy-start | bytes 3145732
  3.1 28.8 %collective-permute-start = (f32[15,32,512]{2,1,0:T(8,128)}, f32[15,32,512]{2,1,0:T(8,128)S(1)}, u32[]{:S(2)}, u32[]{:S(2)}) collective-permute-start(f32[15,32,512]{2,1,0:T(8,128)} %get-tuple-element.61), channel_id=1, source_target_pairs={{0,2},{2,4},{4,6},{6,8},{8,10},{10,12},{12,14},{14,16},{16,18},{18... | collective-permute-start | bytes 2949128 | tf_op jit(solution)/shard_map/ppermute | solution.py:14
  5.2 27.1 %collective-permute-start.1 = (f32[15,32,512]{2,1,0:T(8,128)}, f32[15,32,512]{2,1,0:T(8,128)S(1)}, u32[]{:S(2)}, u32[]{:S(2)}) collective-permute-start(f32[15,32,512]{2,1,0:T(8,128)} %get-tuple-element.62), channel_id=1, source_target_pairs={{2,0},{4,2},{6,4},{8,6},{10,8},{12,10},{14,12},{16,14},{18,16},{20... | collective-permute-start | bytes 2949128 | tf_op jit(solution)/shard_map/ppermute | solution.py:15
  55.8 10.0 %collective-permute-start.3 = (f32[16,7,512]{2,1,0:T(8,128)S(1)}, f32[16,7,512]{2,1,0:T(8,128)S(1)}, u32[]{:S(2)}, u32[]{:S(2)}) collective-permute-start(f32[16,7,512]{2,1,0:T(8,128)S(1)} %get-tuple-element.58), channel_id=1, source_target_pairs={{1,0},{3,2},{5,4},{7,6},{9,8},{11,10},{13,12},{15,14},{17,16},{19,... | collective-permute-start | bytes 688136 | tf_op jit(solution)/shard_map/ppermute | solution.py:15
  57.1 9.9 %collective-permute-start.2 = (f32[16,7,512]{2,1,0:T(8,128)S(1)}, f32[16,7,512]{2,1,0:T(8,128)S(1)}, u32[]{:S(2)}, u32[]{:S(2)}) collective-permute-start(f32[16,7,512]{2,1,0:T(8,128)S(1)} %get-tuple-element.57), channel_id=1, source_target_pairs={{0,1},{2,3},{4,5},{6,7},{8,9},{10,11},{12,13},{14,15},{16,17},{18,... | collective-permute-start | bytes 688136 | tf_op jit(solution)/shard_map/ppermute | solution.py:14
  93.4 25.9 %collective-permute-start.5 = (f32[15,32,512]{2,1,0:T(8,128)S(1)}, f32[15,32,512]{2,1,0:T(8,128)S(1)}, u32[]{:S(2)}, u32[]{:S(2)}) collective-permute-start(f32[15,32,512]{2,1,0:T(8,128)S(1)} %get-tuple-element.56), channel_id=1, source_target_pairs={{0,2},{2,4},{4,6},{6,8},{8,10},{10,12},{12,14},{14,16},{16,18},{18... | collective-permute-start | bytes 2949128 | tf_op jit(solution)/shard_map/ppermute | solution.py:14
  95.3 24.0 %collective-permute-start.4 = (f32[15,32,512]{2,1,0:T(8,128)S(1)}, f32[15,32,512]{2,1,0:T(8,128)S(1)}, u32[]{:S(2)}, u32[]{:S(2)}) collective-permute-start(f32[15,32,512]{2,1,0:T(8,128)S(1)} %get-tuple-element.55), channel_id=1, source_target_pairs={{2,0},{4,2},{6,4},{8,6},{10,8},{12,10},{14,12},{16,14},{18,16},{20... | collective-permute-start | bytes 2949128 | tf_op jit(solution)/shard_map/ppermute | solution.py:15
  142.8 8.3 %collective-permute-start.7 = (f32[16,7,512]{2,1,0:T(8,128)S(1)}, f32[16,7,512]{2,1,0:T(8,128)S(1)}, u32[]{:S(2)}, u32[]{:S(2)}) collective-permute-start(f32[16,7,512]{2,1,0:T(8,128)S(1)} %get-tuple-element.54), channel_id=1, source_target_pairs={{0,1},{2,3},{4,5},{6,7},{8,9},{10,11},{12,13},{14,15},{16,17},{18,... | collective-permute-start | bytes 688136 | tf_op jit(solution)/shard_map/ppermute | solution.py:14
  147.2 8.3 %collective-permute-start.6 = (f32[16,7,512]{2,1,0:T(8,128)S(1)}, f32[16,7,512]{2,1,0:T(8,128)S(1)}, u32[]{:S(2)}, u32[]{:S(2)}) collective-permute-start(f32[16,7,512]{2,1,0:T(8,128)S(1)} %get-tuple-element.53), channel_id=1, source_target_pairs={{1,0},{3,2},{5,4},{7,6},{9,8},{11,10},{13,12},{15,14},{17,16},{19,... | collective-permute-start | bytes 688136 | tf_op jit(solution)/shard_map/ppermute | solution.py:15
  180.9 24.1 %collective-permute-start.9 = (f32[15,32,512]{2,1,0:T(8,128)S(1)}, f32[15,32,512]{2,1,0:T(8,128)S(1)}, u32[]{:S(2)}, u32[]{:S(2)}) collective-permute-start(f32[15,32,512]{2,1,0:T(8,128)S(1)} %get-tuple-element.52), channel_id=1, source_target_pairs={{2,0},{4,2},{6,4},{8,6},{10,8},{12,10},{14,12},{16,14},{18,16},{20... | collective-permute-start | bytes 2949128 | tf_op jit(solution)/shard_map/ppermute | solution.py:15
  182.8 22.1 %collective-permute-start.8 = (f32[15,32,512]{2,1,0:T(8,128)S(1)}, f32[15,32,512]{2,1,0:T(8,128)S(1)}, u32[]{:S(2)}, u32[]{:S(2)}) collective-permute-start(f32[15,32,512]{2,1,0:T(8,128)S(1)} %get-tuple-element.51), channel_id=1, source_target_pairs={{0,2},{2,4},{4,6},{6,8},{8,10},{10,12},{12,14},{14,16},{16,18},{18... | collective-permute-start | bytes 2949128 | tf_op jit(solution)/shard_map/ppermute | solution.py:14
  228.5 8.3 %collective-permute-start.11 = (f32[16,7,512]{2,1,0:T(8,128)S(1)}, f32[16,7,512]{2,1,0:T(8,128)S(1)}, u32[]{:S(2)}, u32[]{:S(2)}) collective-permute-start(f32[16,7,512]{2,1,0:T(8,128)S(1)} %get-tuple-element.50), channel_id=1, source_target_pairs={{1,0},{3,2},{5,4},{7,6},{9,8},{11,10},{13,12},{15,14},{17,16},{19,... | collective-permute-start | bytes 688136 | tf_op jit(solution)/shard_map/ppermute | solution.py:15
  229.8 8.4 %collective-permute-start.10 = (f32[16,7,512]{2,1,0:T(8,128)S(1)}, f32[16,7,512]{2,1,0:T(8,128)S(1)}, u32[]{:S(2)}, u32[]{:S(2)}) collective-permute-start(f32[16,7,512]{2,1,0:T(8,128)S(1)} %get-tuple-element.49), channel_id=1, source_target_pairs={{0,1},{2,3},{4,5},{6,7},{8,9},{10,11},{12,13},{14,15},{16,17},{18,... | collective-permute-start | bytes 688136 | tf_op jit(solution)/shard_map/ppermute | solution.py:14
  264.7 25.9 %collective-permute-start.13 = (f32[15,32,512]{2,1,0:T(8,128)S(1)}, f32[15,32,512]{2,1,0:T(8,128)S(1)}, u32[]{:S(2)}, u32[]{:S(2)}) collective-permute-start(f32[15,32,512]{2,1,0:T(8,128)S(1)} %get-tuple-element.48), channel_id=1, source_target_pairs={{0,2},{2,4},{4,6},{6,8},{8,10},{10,12},{12,14},{14,16},{16,18},{18... | collective-permute-start | bytes 2949128 | tf_op jit(solution)/shard_map/ppermute | solution.py:14
  266.6 24.0 %collective-permute-start.12 = (f32[15,32,512]{2,1,0:T(8,128)S(1)}, f32[15,32,512]{2,1,0:T(8,128)S(1)}, u32[]{:S(2)}, u32[]{:S(2)}) collective-permute-start(f32[15,32,512]{2,1,0:T(8,128)S(1)} %get-tuple-element.47), channel_id=1, source_target_pairs={{2,0},{4,2},{6,4},{8,6},{10,8},{12,10},{14,12},{16,14},{18,16},{20... | collective-permute-start | bytes 2949128 | tf_op jit(solution)/shard_map/ppermute | solution.py:15
  314.2 8.3 %collective-permute-start.15 = (f32[16,7,512]{2,1,0:T(8,128)S(1)}, f32[16,7,512]{2,1,0:T(8,128)S(1)}, u32[]{:S(2)}, u32[]{:S(2)}) collective-permute-start(f32[16,7,512]{2,1,0:T(8,128)S(1)} %get-tuple-element.46), channel_id=1, source_target_pairs={{0,1},{2,3},{4,5},{6,7},{8,9},{10,11},{12,13},{14,15},{16,17},{18,... | collective-permute-start | bytes 688136 | tf_op jit(solution)/shard_map/ppermute | solution.py:14
  318.6 8.3 %collective-permute-start.14 = (f32[16,7,512]{2,1,0:T(8,128)S(1)}, f32[16,7,512]{2,1,0:T(8,128)S(1)}, u32[]{:S(2)}, u32[]{:S(2)}) collective-permute-start(f32[16,7,512]{2,1,0:T(8,128)S(1)} %get-tuple-element.45), channel_id=1, source_target_pairs={{1,0},{3,2},{5,4},{7,6},{9,8},{11,10},{13,12},{15,14},{17,16},{19,... | collective-permute-start | bytes 688136 | tf_op jit(solution)/shard_map/ppermute | solution.py:15
  352.1 24.1 %collective-permute-start.17 = (f32[15,32,512]{2,1,0:T(8,128)S(1)}, f32[15,32,512]{2,1,0:T(8,128)S(1)}, u32[]{:S(2)}, u32[]{:S(2)}) collective-permute-start(f32[15,32,512]{2,1,0:T(8,128)S(1)} %get-tuple-element.44), channel_id=1, source_target_pairs={{2,0},{4,2},{6,4},{8,6},{10,8},{12,10},{14,12},{16,14},{18,16},{20... | collective-permute-start | bytes 2949128 | tf_op jit(solution)/shard_map/ppermute | solution.py:15
  354.1 22.1 %collective-permute-start.16 = (f32[15,32,512]{2,1,0:T(8,128)S(1)}, f32[15,32,512]{2,1,0:T(8,128)S(1)}, u32[]{:S(2)}, u32[]{:S(2)}) collective-permute-start(f32[15,32,512]{2,1,0:T(8,128)S(1)} %get-tuple-element.43), channel_id=1, source_target_pairs={{0,2},{2,4},{4,6},{6,8},{8,10},{10,12},{12,14},{14,16},{16,18},{18... | collective-permute-start | bytes 2949128 | tf_op jit(solution)/shard_map/ppermute | solution.py:14
  399.8 8.3 %collective-permute-start.19 = (f32[16,7,512]{2,1,0:T(8,128)S(1)}, f32[16,7,512]{2,1,0:T(8,128)S(1)}, u32[]{:S(2)}, u32[]{:S(2)}) collective-permute-start(f32[16,7,512]{2,1,0:T(8,128)S(1)} %get-tuple-element.42), channel_id=1, source_target_pairs={{1,0},{3,2},{5,4},{7,6},{9,8},{11,10},{13,12},{15,14},{17,16},{19,... | collective-permute-start | bytes 688136 | tf_op jit(solution)/shard_map/ppermute | solution.py:15
  401.1 8.4 %collective-permute-start.18 = (f32[16,7,512]{2,1,0:T(8,128)S(1)}, f32[16,7,512]{2,1,0:T(8,128)S(1)}, u32[]{:S(2)}, u32[]{:S(2)}) collective-permute-start(f32[16,7,512]{2,1,0:T(8,128)S(1)} %get-tuple-element.41), channel_id=1, source_target_pairs={{0,1},{2,3},{4,5},{6,7},{8,9},{10,11},{12,13},{14,15},{16,17},{18,... | collective-permute-start | bytes 688136 | tf_op jit(solution)/shard_map/ppermute | solution.py:14
  435.9 25.9 %collective-permute-start.21 = (f32[15,32,512]{2,1,0:T(8,128)S(1)}, f32[15,32,512]{2,1,0:T(8,128)S(1)}, u32[]{:S(2)}, u32[]{:S(2)}) collective-permute-start(f32[15,32,512]{2,1,0:T(8,128)S(1)} %get-tuple-element.40), channel_id=1, source_target_pairs={{0,2},{2,4},{4,6},{6,8},{8,10},{10,12},{12,14},{14,16},{16,18},{18... | collective-permute-start | bytes 2949128 | tf_op jit(solution)/shard_map/ppermute | solution.py:14
  437.8 24.0 %collective-permute-start.20 = (f32[15,32,512]{2,1,0:T(8,128)S(1)}, f32[15,32,512]{2,1,0:T(8,128)S(1)}, u32[]{:S(2)}, u32[]{:S(2)}) collective-permute-start(f32[15,32,512]{2,1,0:T(8,128)S(1)} %get-tuple-element.39), channel_id=1, source_target_pairs={{2,0},{4,2},{6,4},{8,6},{10,8},{12,10},{14,12},{16,14},{18,16},{20... | collective-permute-start | bytes 2949128 | tf_op jit(solution)/shard_map/ppermute | solution.py:15
  485.4 8.3 %collective-permute-start.23 = (f32[16,7,512]{2,1,0:T(8,128)S(1)}, f32[16,7,512]{2,1,0:T(8,128)S(1)}, u32[]{:S(2)}, u32[]{:S(2)}) collective-permute-start(f32[16,7,512]{2,1,0:T(8,128)S(1)} %get-tuple-element.38), channel_id=1, source_target_pairs={{0,1},{2,3},{4,5},{6,7},{8,9},{10,11},{12,13},{14,15},{16,17},{18,... | collective-permute-start | bytes 688136 | tf_op jit(solution)/shard_map/ppermute | solution.py:14
  489.8 8.3 %collective-permute-start.22 = (f32[16,7,512]{2,1,0:T(8,128)S(1)}, f32[16,7,512]{2,1,0:T(8,128)S(1)}, u32[]{:S(2)}, u32[]{:S(2)}) collective-permute-start(f32[16,7,512]{2,1,0:T(8,128)S(1)} %get-tuple-element.37), channel_id=1, source_target_pairs={{1,0},{3,2},{5,4},{7,6},{9,8},{11,10},{13,12},{15,14},{17,16},{19,... | collective-permute-start | bytes 688136 | tf_op jit(solution)/shard_map/ppermute | solution.py:15
  523.5 22.9 %collective-permute-start.25 = (f32[15,32,512]{2,1,0:T(8,128)S(1)}, f32[15,32,512]{2,1,0:T(8,128)S(1)}, u32[]{:S(2)}, u32[]{:S(2)}) collective-permute-start(f32[15,32,512]{2,1,0:T(8,128)S(1)} %get-tuple-element.36), channel_id=1, source_target_pairs={{2,0},{4,2},{6,4},{8,6},{10,8},{12,10},{14,12},{16,14},{18,16},{20... | collective-permute-start | bytes 2949128 | tf_op jit(solution)/shard_map/ppermute | solution.py:15
  525.5 20.9 %collective-permute-start.24 = (f32[15,32,512]{2,1,0:T(8,128)S(1)}, f32[15,32,512]{2,1,0:T(8,128)S(1)}, u32[]{:S(2)}, u32[]{:S(2)}) collective-permute-start(f32[15,32,512]{2,1,0:T(8,128)S(1)} %get-tuple-element.35), channel_id=1, source_target_pairs={{0,2},{2,4},{4,6},{6,8},{8,10},{10,12},{12,14},{14,16},{16,18},{18... | collective-permute-start | bytes 2949128 | tf_op jit(solution)/shard_map/ppermute | solution.py:14
  569.9 8.3 %collective-permute-start.27 = (f32[16,7,512]{2,1,0:T(8,128)S(1)}, f32[16,7,512]{2,1,0:T(8,128)S(1)}, u32[]{:S(2)}, u32[]{:S(2)}) collective-permute-start(f32[16,7,512]{2,1,0:T(8,128)S(1)} %get-tuple-element.34), channel_id=1, source_target_pairs={{1,0},{3,2},{5,4},{7,6},{9,8},{11,10},{13,12},{15,14},{17,16},{19,... | collective-permute-start | bytes 688136 | tf_op jit(solution)/shard_map/ppermute | solution.py:15
  571.2 8.4 %collective-permute-start.26 = (f32[16,7,512]{2,1,0:T(8,128)S(1)}, f32[16,7,512]{2,1,0:T(8,128)S(1)}, u32[]{:S(2)}, u32[]{:S(2)}) collective-permute-start(f32[16,7,512]{2,1,0:T(8,128)S(1)} %get-tuple-element.33), channel_id=1, source_target_pairs={{0,1},{2,3},{4,5},{6,7},{8,9},{10,11},{12,13},{14,15},{16,17},{18,... | collective-permute-start | bytes 688136 | tf_op jit(solution)/shard_map/ppermute | solution.py:14
  606.1 25.2 %collective-permute-start.29 = (f32[15,32,512]{2,1,0:T(8,128)S(1)}, f32[15,32,512]{2,1,0:T(8,128)S(1)}, u32[]{:S(2)}, u32[]{:S(2)}) collective-permute-start(f32[15,32,512]{2,1,0:T(8,128)S(1)} %get-tuple-element.32), channel_id=1, source_target_pairs={{0,2},{2,4},{4,6},{6,8},{8,10},{10,12},{12,14},{14,16},{16,18},{18... | collective-permute-start | bytes 2949128 | tf_op jit(solution)/shard_map/ppermute | solution.py:14
  608.0 23.3 %collective-permute-start.28 = (f32[15,32,512]{2,1,0:T(8,128)S(1)}, f32[15,32,512]{2,1,0:T(8,128)S(1)}, u32[]{:S(2)}, u32[]{:S(2)}) collective-permute-start(f32[15,32,512]{2,1,0:T(8,128)S(1)} %get-tuple-element.31), channel_id=1, source_target_pairs={{2,0},{4,2},{6,4},{8,6},{10,8},{12,10},{14,12},{16,14},{18,16},{20... | collective-permute-start | bytes 2949128 | tf_op jit(solution)/shard_map/ppermute | solution.py:15
  654.9 8.1 %collective-permute-start.31 = (f32[16,7,512]{2,1,0:T(8,128)S(1)}, f32[16,7,512]{2,1,0:T(8,128)S(1)}, u32[]{:S(2)}, u32[]{:S(2)}) collective-permute-start(f32[16,7,512]{2,1,0:T(8,128)S(1)} %get-tuple-element.30), channel_id=1, source_target_pairs={{0,1},{2,3},{4,5},{6,7},{8,9},{10,11},{12,13},{14,15},{16,17},{18,... | collective-permute-start | bytes 688136 | tf_op jit(solution)/shard_map/ppermute | solution.py:14
  659.1 8.3 %collective-permute-start.30 = (f32[16,7,512]{2,1,0:T(8,128)S(1)}, f32[16,7,512]{2,1,0:T(8,128)S(1)}, u32[]{:S(2)}, u32[]{:S(2)}) collective-permute-start(f32[16,7,512]{2,1,0:T(8,128)S(1)} %get-tuple-element.29), channel_id=1, source_target_pairs={{1,0},{3,2},{5,4},{7,6},{9,8},{11,10},{13,12},{15,14},{17,16},{19,... | collective-permute-start | bytes 688136 | tf_op jit(solution)/shard_map/ppermute | solution.py:15
where the time goes:
time: 706 us; the launch traced here: 694 us
  other arithmetic  410 us (58%)
  waiting for transfers between devices  167 us (24%)
  starting transfers between devices  88 us (12%)
  local copies, waits for them, and re-layouts  19.9 us (3%)
  between operations  8.36 us (1%)
    add x16, other arithmetic, correlate_padded(): total = term if total is None else total + term  283 us
    ppermute x16, waiting for transfers between devices, with_halo(): before = lax.ppermute(last, axis, up)  95.7 us
    ppermute x16, waiting for transfers between devices, with_halo(): after = lax.ppermute(initial, axis, down)  71.2 us
    div x4, other arithmetic, on_device(): ratio = recorded / blurred  57.4 us
    mul x4, other arithmetic, on_device(): current = current * blur(ratio, weights_z, weights_y, weights_x, True)  53.8 us
    ppermute x16, starting transfers between devices, with_halo(): before = lax.ppermute(last, axis, up)  52.7 us
    ppermute x16, starting transfers between devices, with_halo(): after = lax.ppermute(initial, axis, down)  35.3 us
  transfers between devices with their start and end apart: 32, of which 23 were waited for; matrix products, arithmetic and copies ran while one was open for 5% of the time, Pallas kernels for 0%

commit v1 on v0

--- a/solution.py
+++ b/solution.py
@@ -1,7 +1,15 @@
+import functools
 import jax
 import jax.numpy as jnp
 from jax import lax
+from jax.experimental import pallas as pl
+from jax.experimental.pallas import tpu as pltpu
 from jax.sharding import PartitionSpec as P
+
+MESH = pl.DeviceIdType.MESH
+RZ = 15
+RL = 7
+LANES = 128
 
 
 def with_halo(value, sides, width):
@@ -34,29 +42,392 @@
 
 
 def blur(field, weights_z, weights_y, weights_x, flipped):
-    planes = field.shape[0]
-    rows = field.shape[1]
-    padded = with_halo(field, (("gz", 0),), 15)
-    result = correlate_padded(padded, weights_z, 0, 15, planes, flipped)
-    widened = with_halo(result, (("gy", 1),), 7)
-    result = correlate_padded(widened, weights_y, 1, 7, rows, flipped)
-    result = jnp.pad(result, ((0, 0), (0, 0), (7, 7)))
-    return correlate_padded(result, weights_x, 2, 7, field.shape[2], flipped)
-
-
-def on_device(estimate, measured, psf_z, psf_y, psf_x, extents, order):
+    padded = with_halo(field, (("gz", 0),), RZ)
+    result = correlate_padded(padded, weights_z, 0, RZ, field.shape[0], flipped)
+    widened = with_halo(result, (("gy", 1),), RL)
+    result = correlate_padded(widened, weights_y, 1, RL, field.shape[1], flipped)
+    result = jnp.pad(result, ((0, 0), (0, 0), (RL, RL)))
+    return correlate_padded(result, weights_x, 2, RL, field.shape[2], flipped)
+
+
+def general(estimate, measured, psf_z, psf_y, psf_x, extents, order):
     current = estimate
     for position in range(measured.shape[0]):
         view = order[position]
         radii = (extents[view] - 1) // 2
-        weights_z = line_taps(psf_z[view], radii[0], 15)
-        weights_y = line_taps(psf_y[view], radii[1], 7)
-        weights_x = line_taps(psf_x[view], radii[2], 7)
+        weights_z = line_taps(psf_z[view], radii[0], RZ)
+        weights_y = line_taps(psf_y[view], radii[1], RL)
+        weights_x = line_taps(psf_x[view], radii[2], RL)
         recorded = lax.dynamic_index_in_dim(measured, view, 0, keepdims=False)
         blurred = blur(current, weights_z, weights_y, weights_x, False)
         ratio = recorded / blurred
         current = current * blur(ratio, weights_z, weights_y, weights_x, True)
     return current
+
+
+def place():
+    g = lax.axis_index("gz")
+    w = lax.axis_index("gy")
+    return g // 4, (g // 2) % 2, g % 2, w
+
+
+def slab_of(a, w):
+    return 2 * a + lax.rem(w + a, 2)
+
+
+def group_peers():
+    h, a, c, w = place()
+    peers = []
+    for k in range(1, 8):
+        da, dc, dw = k // 4, (k // 2) % 2, k % 2
+        device = (4 * h + 2 * lax.rem(a + da, 2) + lax.rem(c + dc, 2), lax.rem(w + dw, 2))
+        peers.append(device)
+    return peers
+
+
+def spread_kernel(nz, ny, back, n, *refs):
+    srcs, dsts = refs[:n], refs[n:2 * n]
+    send, recv, local = refs[2 * n:]
+    h, a, c, w = place()
+    barrier = pltpu.get_barrier_semaphore()
+    for device in group_peers():
+        pl.semaphore_signal(barrier, inc=1, device_id=device, device_id_type=MESH)
+    pl.semaphore_wait(barrier, 7)
+    for phase in ("start", "wait"):
+        for i in range(n):
+            for k in range(4):
+                da, dw = k // 2, k % 2
+                if not back:
+                    ta, tw = lax.rem(c + da, 2), lax.rem(w + dw, 2)
+                    device = (4 * h + 2 * ta + a, tw)
+                    x0 = pl.multiple_of(LANES * slab_of(ta, tw), LANES)
+                    src = srcs[i].at[:, :, pl.ds(x0, LANES)]
+                    dst = dsts[i].at[pl.ds(nz * c, nz), pl.ds(pl.multiple_of(ny * w, 8), ny), :]
+                    mine = jnp.logical_and(c == a, jnp.logical_and(ta == a, tw == w))
+                else:
+                    tc, tw = lax.rem(a + da, 2), lax.rem(w + dw, 2)
+                    device = (4 * h + 2 * c + tc, tw)
+                    x0 = pl.multiple_of(LANES * slab_of(a, w), LANES)
+                    src = srcs[i].at[pl.ds(nz * tc, nz), pl.ds(pl.multiple_of(ny * tw, 8), ny), :]
+                    dst = dsts[i].at[:, :, pl.ds(x0, LANES)]
+                    mine = jnp.logical_and(c == a, jnp.logical_and(tc == c, tw == w))
+                remote = pltpu.make_async_remote_copy(
+                    src_ref=src, dst_ref=dst, send_sem=send.at[i, k], recv_sem=recv.at[i, k],
+                    device_id=device, device_id_type=MESH)
+                if phase == "start":
+                    @pl.when(mine)
+                    def _():
+                        pltpu.make_async_copy(src, dst, local.at[i]).start()
+
+                    @pl.when(jnp.logical_not(mine))
+                    def _():
+                        remote.start()
+                else:
+                    @pl.when(mine)
+                    def _():
+                        pltpu.make_async_copy(src, dst, local.at[i]).wait()
+
+                    @pl.when(jnp.logical_not(mine))
+                    def _():
+                        remote.wait()
+
+
+def spread(arrays, nz, ny, nx, back, cid):
+    n = len(arrays)
+    shape = (nz, ny, nx) if back else (2 * nz, 2 * ny, LANES)
+    out = pl.pallas_call(
+        functools.partial(spread_kernel, nz, ny, back, n),
+        out_shape=[jax.ShapeDtypeStruct(shape, jnp.float32)] * n,
+        in_specs=[pl.BlockSpec(memory_space=pl.ANY)] * n,
+        out_specs=[pl.BlockSpec(memory_space=pl.ANY)] * n,
+        scratch_shapes=[
+            pltpu.SemaphoreType.DMA((n, 4)),
+            pltpu.SemaphoreType.DMA((n, 4)),
+            pltpu.SemaphoreType.DMA((n,)),
+        ],
+        compiler_params=pltpu.CompilerParams(collective_id=cid, has_side_effects=True),
+    )(*arrays)
+    return out
+
+
+def split(value):
+    hi = value.astype(jnp.bfloat16)
+    lo = (value - hi.astype(jnp.float32)).astype(jnp.bfloat16)
+    return hi, lo
+
+
+CHUNKS = 4
+
+
+def blur_kernel(divide, chain, f, other, wz, ym, xm, xe, out,
+                below, above, zb, pack_l, pack_r, got_l, got_r, zs, zr, xs, xr):
+    planes, rows, _ = f.shape
+    h, a, c, w = place()
+    zi = 2 * h + c
+    s = slab_of(a, w)
+    has_dn, has_up = zi > 0, zi < chain - 1
+    has_l, has_r = s > 0, s < 3
+
+    def z_dev(i):
+        return (4 * (i // 2) + 2 * a + lax.rem(i, 2), w)
+
+    def x_dev(i):
+        b = i // 2
+        return (4 * h + 2 * b + c, lax.rem(i + b, 2))
+
+    up, dn = z_dev(lax.rem(zi + 1, chain)), z_dev(lax.rem(zi + chain - 1, chain))
+    lf, rt = x_dev(lax.rem(s + 3, 4)), x_dev(lax.rem(s + 1, 4))
+
+    barrier = pltpu.get_barrier_semaphore()
+    for there, device in ((has_up, up), (has_dn, dn), (has_l, lf), (has_r, rt)):
+        @pl.when(there)
+        def _():
+            pl.semaphore_signal(barrier, inc=1, device_id=device, device_id_type=MESH)
+    peers = sum(there.astype(jnp.int32) for there in (has_up, has_dn, has_l, has_r))
+    pl.semaphore_wait(barrier, peers)
+
+    part = rows // CHUNKS
+
+    def z_copy(side, j):
+        ys = pl.ds(j * part, part)
+        if side == 0:
+            return pltpu.make_async_remote_copy(
+                src_ref=f.at[pl.ds(planes - RZ, RZ), ys, :], dst_ref=below.at[:, ys, :],
+                send_sem=zs.at[0, j], recv_sem=zr.at[0, j], device_id=up, device_id_type=MESH)
+        return pltpu.make_async_remote_copy(
+            src_ref=f.at[pl.ds(0, RZ), ys, :], dst_ref=above.at[:, ys, :],
+            send_sem=zs.at[1, j], recv_sem=zr.at[1, j], device_id=dn, device_id_type=MESH)
+
+    def x_copy(side):
+        if side == 0:
+            return pltpu.make_async_remote_copy(
+                src_ref=pack_r, dst_ref=got_l,
+                send_sem=xs.at[0], recv_sem=xr.at[0], device_id=rt, device_id_type=MESH)
+        return pltpu.make_async_remote_copy(
+            src_ref=pack_l, dst_ref=got_r,
+            send_sem=xs.at[1], recv_sem=xr.at[1], device_id=lf, device_id_type=MESH)
+
+    for j in range(CHUNKS):
+        @pl.when(has_up)
+        def _():
+            z_copy(0, j).start()
+
+        @pl.when(has_dn)
+        def _():
+            z_copy(1, j).start()
+
+    @pl.when(jnp.logical_not(has_dn))
+    def _():
+        below[...] = jnp.zeros_like(below)
+
+    @pl.when(jnp.logical_not(has_up))
+    def _():
+        above[...] = jnp.zeros_like(above)
+
+    @pl.when(jnp.logical_not(has_l))
+    def _():
+        got_l[...] = jnp.zeros_like(got_l)
+
+    @pl.when(jnp.logical_not(has_r))
+    def _():
+        got_r[...] = jnp.zeros_like(got_r)
+
+    half = 16
+
+    def z_tile(t, carry):
+        ys = pl.ds(pl.multiple_of(8 * t, 8), 8)
+        taps = [wz[k] for k in range(2 * RZ + 1)]
+        for first in range(0, planes, half):
+            acc = [None] * half
+            for p in range(first, first + half + 2 * RZ):
+                if p < RZ:
+                    v = below[p, ys, :]
+                elif p < RZ + planes:
+                    v = f[p - RZ, ys, :]
+                else:
+                    v = above[p - RZ - planes, ys, :]
+                for o in range(half):
+                    k = p - first - o
+                    if 0 <= k <= 2 * RZ:
+                        term = taps[k] * v
+                        acc[o] = term if acc[o] is None else acc[o] + term
+            for o in range(half):
+                zb[first + o, ys, :] = acc[o]
+        return carry
+
+    for j in range(CHUNKS):
+        @pl.when(has_dn)
+        def _():
+            z_copy(0, j).wait_recv()
+
+        @pl.when(has_up)
+        def _():
+            z_copy(1, j).wait_recv()
+
+        lax.fori_loop(j * part // 8, (j + 1) * part // 8, z_tile, 0)
+
+    for j in range(CHUNKS):
+        @pl.when(has_up)
+        def _():
+            z_copy(0, j).wait_send()
+
+        @pl.when(has_dn)
+        def _():
+            z_copy(1, j).wait_send()
+
+    lane = lax.broadcasted_iota(jnp.int32, (rows, LANES), 1)
+    per = LANES // 8
+
+    for q in range(planes // per):
+        packed_l = packed_r = None
+        for k in range(0, per, 2):
+            p = q * per + k
+            his, los = zip(*(split(zb[p + i]) for i in range(2)))
+            hi = jnp.concatenate(his, axis=1)
+            lo = jnp.concatenate(los, axis=1)
+            got = jnp.dot(ym[...], jnp.concatenate([hi, lo, hi, lo], axis=0),
+                          preferred_element_type=jnp.float32)
+            for i in range(2):
+                value = got[:, i * LANES:(i + 1) * LANES]
+                zb[p + i] = value
+                at = 8 * (k + i)
+                left = value if at == 0 else pltpu.roll(value, at, 1)
+                right = pltpu.roll(value, (at + 8) % LANES, 1) if at + 8 < LANES else value
+                if packed_l is None:
+                    packed_l, packed_r = left, right
+                else:
+                    packed_l = jnp.where(lane >= at, left, packed_l)
+                    packed_r = jnp.where(lane >= at, right, packed_r)
+        pack_l[q] = packed_l
+        pack_r[q] = packed_r
+
+    @pl.when(has_r)
+    def _():
+        x_copy(0).start()
+
+    @pl.when(has_l)
+    def _():
+        x_copy(1).start()
+
+    step = 4
+    for p in range(0, planes, step):
+        hi, lo = split(zb[p:p + step].reshape(step * rows, LANES))
+        got = jnp.dot(jnp.concatenate([hi, lo], axis=1), xm[...], preferred_element_type=jnp.float32)
+        zb[p:p + step] = (got[:, :LANES] + got[:, LANES:]).reshape(step, rows, LANES)
+
+    @pl.when(has_l)
+    def _():
+        x_copy(0).wait_recv()
+
+    @pl.when(has_r)
+    def _():
+        x_copy(1).wait_recv()
+
+    for p in range(0, planes, step):
+        edges = []
+        for i in range(step):
+            q, k = divmod(p + i, per)
+            left, right = got_l[q], got_r[q]
+            at = 8 * k
+            left = left if at == 0 else pltpu.roll(left, LANES - at, 1)
+            right = right if at == 8 else pltpu.roll(right, (LANES - at + 8) % LANES, 1)
+            edges.append(jnp.where(lane < 8, left, right))
+        hi, lo = split(jnp.concatenate(edges, axis=0))
+        got = jnp.dot(jnp.concatenate([hi, lo], axis=1), xe[...], preferred_element_type=jnp.float32)
+        value = zb[p:p + step] + (got[:, :LANES] + got[:, LANES:]).reshape(step, rows, LANES)
+        if divide:
+            out[p:p + step] = other[p:p + step] / value
+        else:
+            out[p:p + step] = other[p:p + step] * value
+
+    @pl.when(has_r)
+    def _():
+        x_copy(0).wait_send()
+
+    @pl.when(has_l)
+    def _():
+        x_copy(1).wait_send()
+
+
+def slab_blur(f, other, wz, ym, xm, xe, divide, chain):
+    planes, rows, _ = f.shape
+    vmem = pl.BlockSpec(memory_space=pltpu.VMEM)
+    packs = pltpu.VMEM((planes * 8 // LANES, rows, LANES), jnp.float32)
+    return pl.pallas_call(
+        functools.partial(blur_kernel, divide, chain),
+        out_shape=jax.ShapeDtypeStruct(f.shape, jnp.float32),
+        in_specs=[vmem] * 6,
+        out_specs=vmem,
+        scratch_shapes=[
+            pltpu.VMEM((RZ, rows, LANES), jnp.float32),
+            pltpu.VMEM((RZ, rows, LANES), jnp.float32),
+            pltpu.VMEM((planes, rows, LANES), jnp.float32),
+            packs, packs, packs, packs,
+            pltpu.SemaphoreType.DMA((2, CHUNKS)),
+            pltpu.SemaphoreType.DMA((2, CHUNKS)),
+            pltpu.SemaphoreType.DMA((2,)),
+            pltpu.SemaphoreType.DMA((2,)),
+        ],
+        compiler_params=pltpu.CompilerParams(
+            collective_id=3 if divide else 4, has_side_effects=True),
+    )(f, other, wz, ym, xm, xe)
+
+
+def halves(value):
+    hi = lax.reduce_precision(value, 8, 7)
+    return hi.astype(jnp.bfloat16), (value - hi).astype(jnp.bfloat16)
+
+
+def band(weights, source, target, reach):
+    which = source[:, None] - target[None, :] + reach
+    total = jnp.zeros((weights.shape[0],) + which.shape, jnp.float32)
+    for k in range(2 * reach + 1):
+        total = jnp.where(which == k, weights[:, k][:, None, None], total)
+    return total
+
+
+def all_taps(profiles, radii, reach):
+    offsets = jnp.abs(jnp.arange(2 * reach + 1, dtype=jnp.int32) - reach)
+    kept = jnp.where(offsets[None] <= radii[:, None], profiles, 0.0)
+    taps = kept / jnp.sum(kept, axis=1, keepdims=True)
+    return jnp.stack([taps, taps[:, ::-1]], axis=1).reshape(-1, 2 * reach + 1)
+
+
+def slabs(chain, estimate, measured, psf_z, psf_y, psf_x, extents, order):
+    views, nz, ny, nx = measured.shape
+    rows = 2 * ny
+    radii = ((extents - 1) // 2)[order]
+    wz = all_taps(psf_z[order], radii[:, 0], RZ)
+    wy = all_taps(psf_y[order], radii[:, 1], RL)
+    wx = all_taps(psf_x[order], radii[:, 2], RL)
+    wz = jnp.broadcast_to(wz[:, :, None, None], wz.shape + (8, LANES))
+    cells = jnp.arange(rows, dtype=jnp.int32)
+    hi, lo = halves(band(wy, cells, cells, RL).swapaxes(1, 2))
+    ym = jnp.concatenate([hi, hi, lo, lo], axis=2)
+    cells = jnp.arange(LANES, dtype=jnp.int32)
+    hi, lo = halves(band(wx, cells, cells, RL))
+    xm = jnp.concatenate([jnp.concatenate([hi, lo], axis=2)] * 2, axis=1)
+    edge = jnp.where(cells < 8, cells - 8, jnp.where(cells < 16, LANES - 8 + cells, -4 * LANES))
+    hi, lo = halves(band(wx, edge, cells, RL))
+    xe = jnp.concatenate([jnp.concatenate([hi, lo], axis=2)] * 2, axis=1)
+    recorded = [lax.dynamic_index_in_dim(measured, order[p], 0, keepdims=False) for p in range(views)]
+    moved = spread([estimate] + recorded, nz, ny, nx, False, 1)
+    current = moved[0]
+    for p in range(views):
+        i = 2 * p
+        ratio = slab_blur(current, moved[1 + p], wz[i], ym[i], xm[i], xe[i], True, chain)
+        i = i + 1
+        current = slab_blur(ratio, current, wz[i], ym[i], xm[i], xe[i], False, chain)
+    return spread([current], nz, ny, nx, True, 2)[0]
+
+
+def on_device(estimate, measured, psf_z, psf_y, psf_x, extents, order):
+    n_z, n_y = lax.axis_size("gz"), lax.axis_size("gy")
+    nz, ny, nx = estimate.shape
+    fits = n_y == 2 and n_z % 4 == 0 and nx == 4 * LANES and nz == 16 and 2 * ny == 64
+    if fits:
+        return slabs(n_z // 2, estimate, measured, psf_z, psf_y, psf_x, extents, order)
+    return general(estimate, measured, psf_z, psf_y, psf_x, extents, order)
 
 
 def solution(mesh):

time: 706 us -> 247 us (0.35); the launches traced: 694 us -> 244 us
  other arithmetic: 410 us -> 6.79 us
  Pallas kernels: 0 us -> 208 us
  waiting for transfers between devices: 167 us -> 0 us
  starting transfers between devices: 88 us -> 0 us
    add x16 -> x0, other arithmetic: 283 us -> none  [correlate_padded(): total = term if total is None else total + term]
    pallas_call x0 -> x10, Pallas kernels: none -> 208 us  [the longest x8 132 us: slab_blur(): pl.pallas_call(functools.partial(blur_kernel, divide, chain), out_shape=j...]
    ppermute x32 -> x0, waiting for transfers between devices: 167 us -> none  [the longest x16 95.7 us: with_halo(): before = lax.ppermute(last, axis, up)]
    ppermute x32 -> x0, starting transfers between devices: 88 us -> none  [the longest x16 52.7 us: with_halo(): before = lax.ppermute(last, axis, up)]
    div x14 -> x4, other arithmetic: 65 us -> 0.3 us  [all_taps(): taps = kept / jnp.sum(kept, axis=1, keepdims=True)]
    mul x4 -> x0, other arithmetic: 53.8 us -> none  [on_device(): current = current * blur(ratio, weights_z, weights_y, weights_x, True)]
    slice x37 -> x4, local copies, waits for them, and re-layouts: 19.5 us -> 2.54 us  [the longest x1 1.47 us: slabs(): order[p]]
    reduce_sum x2, other arithmetic: 8.92 us -> 0.39 us  [all_taps(): taps = kept / jnp.sum(kept, axis=1, keepdims=True)]
  transfers between devices with their start and end apart: 32 -> 0, of which waited for: 23 -> 0; matrix products, arithmetic and copies ran while one was open for 5% -> 0% of each run, Pallas kernels for 0% -> 0%
where the time goes in v1:
time: 247 us; the launch traced here: 244 us
  Pallas kernels  208 us (84%)
  local copies, waits for them, and re-layouts  20.5 us (8%)
  between operations  7.96 us (3%)
  other arithmetic  6.79 us (3%)
    pallas_call x8, Pallas kernels, slab_blur(): pl.pallas_call(functools.partial(blur_kernel, divide, chain), out_shape=j...  132 us
    pallas_call x2, Pallas kernels, spread(): pl.pallas_call(functools.partial(spread_kernel, nz, ny, back, n), out_sha...  76.7 us
    broadcast_in_dim x9, local copies, waits for them, and re-layouts, slabs(): wz = jnp.broadcast_to(wz[:, :, None, None], wz.shape + (8, LANES))  5.99 us
    convert_element_type x6, other arithmetic, halves(): return (hi.astype(jnp.bfloat16), (value - hi).astype(jnp.bfloat16))  5.07 us

profile of v1, /device:TPU:20, one launch (start us, length us, event | category | flops | bytes accessed | tf_op | source)
XLA Modules:
  0.0 243.6 jit_solution(6899898307915200893)
XLA Ops:
  0.0 1.5 fusion.59
  9.1 4.5 %dynamic-slice_bitcast_fusion = (f32[16,32,512]{2,1,0:T(8,128)}, f32[16,32,512]{2,1,0:T(8,128)}, f32[16,32,512]{2,1,0:T(8,128)}, f32[16,32,512]{2,1,0:T(8,128)}) fusion(f32[4,16,32,512]{3,2,1,0:T(8,128)} %param.8, s32[]{:T(128)S(6)} %select_n.289, s32[]{:T(128)S(6)} %select_n.287, s32[]{:T(128)S(6)} %select_n.286, s32[]{:T(128)S(6)} %select_n.288), kind=kLoop, calls=%fused_computation.6 | loop fusion | bytes 8388624 | tf_op jit(solution)/shard_map/jit(dynamic_index_in_dim)/squeeze | solution.py:413
  13.6 61.1 %shard_map.73 = (f32[32,64,128]{2,1,0:T(8,128)}, f32[32,64,128]{2,1,0:T(8,128)}, f32[32,64,128]{2,1,0:T(8,128)}, f32[32,64,128]{2,1,0:T(8,128)}, f32[32,64,128]{2,1,0:T(8,128)}) custom-call(f32[16,32,512]{2,1,0:T(8,128)} %refs_0_.1, f32[16,32,512]{2,1,0:T(8,128)} %get-tuple-element.52.refs_1_, f32[16,32,512]{2,1,0:T(8,128)} %get-tuple-element.51.refs_2_, ...), custom_call_target="tpu_custom_call" | custom-call | tf_op jit(solution)/shard_map/pallas_call | solution.py:138
  74.7 0.6 gather_fusion.1
  75.3 0.6 gather_fusion
  75.9 0.2 slice_reduce_fusion.30
  76.1 0.2 fusion.54
  76.3 0.1 rev.9
  76.5 0.8 broadcast_in_dim.478.wz
  77.3 0.6 gather_fusion.3
  77.9 0.6 gather_fusion.2
  78.5 0.2 fusion.58
  78.7 0.1 fusion.57
  78.7 0.1 rev.10
  78.8 0.1 fusion.49
  78.9 0.1 rev.11
  79.0 0.4 slice_reduce_fusion.29
  79.7 0.5 fusion.2
  80.2 0.5 reduce-precision_convert_fusion.2
  80.6 0.2 pad_maximum_fusion
  80.8 0.7 slice_bitcast_fusion.16
  81.6 0.4 slice_reduce_fusion.14
  82.3 1.0 fusion
  83.3 1.0 reduce-precision_convert_fusion.1
  84.3 0.1 maximum_maximum_fusion
  84.4 0.9 slice_bitcast_fusion.1
  85.4 0.2 fusion.17
  85.6 1.0 fusion.1
  86.7 1.0 reduce-precision_convert_fusion
  87.7 0.1 maximum_maximum_fusion.1
  87.8 1.0 slice_bitcast_fusion
  88.8 17.4 %shard_map.74.f = f32[32,64,128]{2,1,0:T(8,128)} custom-call(f32[32,64,128]{2,1,0:T(8,128)} %get-tuple-element.10.f.other, f32[32,64,128]{2,1,0:T(8,128)} %get-tuple-element.11.other, f32[31,8,128]{2,1,0:T(8,128)} %broadcast_in_dim.478.wz, bf16[64,256]{1,0:T(8,128)(2,1)} %get-tuple-element.77.ym, bf16[256,256]{1,0:T(8,128)(2,1)} %get-tuple-element.69.xm, ...), custom_call_target="tpu_custom_call" | custom-call | tf_op jit(solution)/shard_map/pallas_call | solution.py:356
  106.2 0.7 broadcast_in_dim.589.wz
  107.0 15.4 %shard_map.75.f.other = f32[32,64,128]{2,1,0:T(8,128)} custom-call(f32[32,64,128]{2,1,0:T(8,128)} %shard_map.74.f, f32[32,64,128]{2,1,0:T(8,128)} %get-tuple-element.10.f.other, f32[31,8,128]{2,1,0:T(8,128)} %broadcast_in_dim.589.wz, bf16[64,256]{1,0:T(8,128)(2,1)} %get-tuple-element.76.ym, bf16[256,256]{1,0:T(8,128)(2,1)} %get-tuple-element.68.xm, ...), custom_call_target="tpu_custom_call" | custom-call | tf_op jit(solution)/shard_map/pallas_call | solution.py:356
  122.4 0.7 broadcast_in_dim.591.wz
  123.1 17.6 %shard_map.76.f = f32[32,64,128]{2,1,0:T(8,128)} custom-call(f32[32,64,128]{2,1,0:T(8,128)} %shard_map.75.f.other, f32[32,64,128]{2,1,0:T(8,128)} %get-tuple-element.12.other, f32[31,8,128]{2,1,0:T(8,128)} %broadcast_in_dim.591.wz, bf16[64,256]{1,0:T(8,128)(2,1)} %get-tuple-element.75.ym, bf16[256,256]{1,0:T(8,128)(2,1)} %get-tuple-element.67.xm, ...), custom_call_target="tpu_custom_call" | custom-call | tf_op jit(solution)/shard_map/pallas_call | solution.py:356
  140.8 0.7 broadcast_in_dim.593.wz
  141.5 15.2 %shard_map.77.f.other = f32[32,64,128]{2,1,0:T(8,128)} custom-call(f32[32,64,128]{2,1,0:T(8,128)} %shard_map.76.f, f32[32,64,128]{2,1,0:T(8,128)} %shard_map.75.f.other, f32[31,8,128]{2,1,0:T(8,128)} %broadcast_in_dim.593.wz, bf16[64,256]{1,0:T(8,128)(2,1)} %get-tuple-element.74.ym, bf16[256,256]{1,0:T(8,128)(2,1)} %get-tuple-element.66.xm, ...), custom_call_target="tpu_custom_call" | custom-call | tf_op jit(solution)/shard_map/pallas_call | solution.py:356
  156.7 0.7 broadcast_in_dim.595.wz
  157.5 17.7 %shard_map.78.f = f32[32,64,128]{2,1,0:T(8,128)} custom-call(f32[32,64,128]{2,1,0:T(8,128)} %shard_map.77.f.other, f32[32,64,128]{2,1,0:T(8,128)} %get-tuple-element.13.other, f32[31,8,128]{2,1,0:T(8,128)} %broadcast_in_dim.595.wz, bf16[64,256]{1,0:T(8,128)(2,1)} %get-tuple-element.73.ym, bf16[256,256]{1,0:T(8,128)(2,1)} %get-tuple-element.65.xm, ...), custom_call_target="tpu_custom_call" | custom-call | tf_op jit(solution)/shard_map/pallas_call | solution.py:356
  175.1 0.7 broadcast_in_dim.597.wz
  175.9 15.3 %shard_map.79.f.other = f32[32,64,128]{2,1,0:T(8,128)} custom-call(f32[32,64,128]{2,1,0:T(8,128)} %shard_map.78.f, f32[32,64,128]{2,1,0:T(8,128)} %shard_map.77.f.other, f32[31,8,128]{2,1,0:T(8,128)} %broadcast_in_dim.597.wz, bf16[64,256]{1,0:T(8,128)(2,1)} %get-tuple-element.72.ym, bf16[256,256]{1,0:T(8,128)(2,1)} %get-tuple-element.64.xm, ...), custom_call_target="tpu_custom_call" | custom-call | tf_op jit(solution)/shard_map/pallas_call | solution.py:356
  191.2 0.7 broadcast_in_dim.599.wz
  191.9 17.6 %shard_map.80.f = f32[32,64,128]{2,1,0:T(8,128)} custom-call(f32[32,64,128]{2,1,0:T(8,128)} %shard_map.79.f.other, f32[32,64,128]{2,1,0:T(8,128)} %get-tuple-element.14.other, f32[31,8,128]{2,1,0:T(8,128)} %broadcast_in_dim.599.wz, bf16[64,256]{1,0:T(8,128)(2,1)} %get-tuple-element.71.ym, bf16[256,256]{1,0:T(8,128)(2,1)} %get-tuple-element.63.xm, ...), custom_call_target="tpu_custom_call" | custom-call | tf_op jit(solution)/shard_map/pallas_call | solution.py:356
  209.5 0.7 broadcast_in_dim.601.wz
  210.3 15.4 %shard_map.81.refs_0_ = f32[32,64,128]{2,1,0:T(8,128)} custom-call(f32[32,64,128]{2,1,0:T(8,128)} %shard_map.80.f, f32[32,64,128]{2,1,0:T(8,128)} %shard_map.79.f.other, f32[31,8,128]{2,1,0:T(8,128)} %broadcast_in_dim.601.wz, bf16[64,256]{1,0:T(8,128)(2,1)} %get-tuple-element.70.ym, bf16[256,256]{1,0:T(8,128)(2,1)} %get-tuple-element.62.xm, ...), custom_call_target="tpu_custom_call" | custom-call | tf_op jit(solution)/shard_map/pallas_call | solution.py:356
  225.7 15.6 %shard_map.82 = f32[16,32,512]{2,1,0:T(8,128)} custom-call(f32[32,64,128]{2,1,0:T(8,128)} %shard_map.81.refs_0_), custom_call_target="tpu_custom_call" | custom-call | tf_op jit(solution)/shard_map/pallas_call | solution.py:138
  241.3 2.3 copy.14
  (40 shorter events, 0.6 us)
Async XLA Ops:
  0.0 74.7 %copy-start = (f32[4,31]{1,0:T(4,128)S(1)}, f32[4,31]{1,0:T(4,128)}, u32[]{:S(2)}) copy-start(f32[4,31]{1,0:T(4,128)} %param.9) | copy-start | bytes 1492
  13.5 61.1 %copy-start.3 = (s32[4]{0:T(128)S(1)}, s32[4]{0:T(128)}, u32[]{:S(2)}) copy-start(s32[4]{0:T(128)} %param.13) | copy-start | bytes 52
  13.5 61.7 %copy-start.4 = (s32[4,3]{1,0:T(4,128)S(1)}, s32[4,3]{1,0:T(4,128)}, u32[]{:S(2)}) copy-start(s32[4,3]{1,0:T(4,128)} %param.12) | copy-start | bytes 148
  13.6 63.8 %copy-start.1 = (f32[4,15]{1,0:T(4,128)S(1)}, f32[4,15]{1,0:T(4,128)}, u32[]{:S(2)}) copy-start(f32[4,15]{1,0:T(4,128)} %param.11) | copy-start | bytes 724
  13.6 64.3 %copy-start.2 = (f32[4,15]{1,0:T(4,128)S(1)}, f32[4,15]{1,0:T(4,128)}, u32[]{:S(2)}) copy-start(f32[4,15]{1,0:T(4,128)} %param.10) | copy-start | bytes 724

commit v2 on v1

--- a/solution.py
+++ b/solution.py
@@ -85,69 +85,155 @@
     return peers
 
 
-def spread_kernel(nz, ny, back, n, *refs):
-    srcs, dsts = refs[:n], refs[n:2 * n]
-    send, recv, local = refs[2 * n:]
+def spread_kernel(nz, ny, back, srcs, dst_ref, send, recv, local, between=None):
     h, a, c, w = place()
     barrier = pltpu.get_barrier_semaphore()
     for device in group_peers():
         pl.semaphore_signal(barrier, inc=1, device_id=device, device_id_type=MESH)
     pl.semaphore_wait(barrier, 7)
     for phase in ("start", "wait"):
-        for i in range(n):
-            for k in range(4):
-                da, dw = k // 2, k % 2
-                if not back:
-                    ta, tw = lax.rem(c + da, 2), lax.rem(w + dw, 2)
-                    device = (4 * h + 2 * ta + a, tw)
-                    x0 = pl.multiple_of(LANES * slab_of(ta, tw), LANES)
-                    src = srcs[i].at[:, :, pl.ds(x0, LANES)]
-                    dst = dsts[i].at[pl.ds(nz * c, nz), pl.ds(pl.multiple_of(ny * w, 8), ny), :]
-                    mine = jnp.logical_and(c == a, jnp.logical_and(ta == a, tw == w))
+        for k in range(4):
+            da, dw = k // 2, k % 2
+            if not back:
+                ta, tw = lax.rem(c + da, 2), lax.rem(w + dw, 2)
+                device = (4 * h + 2 * ta + a, tw)
+                x0 = pl.multiple_of(LANES * slab_of(ta, tw), LANES)
+                src = srcs.at[:, :, pl.ds(x0, LANES)]
+                dst = dst_ref.at[pl.ds(nz * c, nz), pl.ds(pl.multiple_of(ny * w, 8), ny), :]
+            else:
+                tc, tw = lax.rem(a + da, 2), lax.rem(w + dw, 2)
+                device = (4 * h + 2 * c + tc, tw)
+                x0 = pl.multiple_of(LANES * slab_of(a, w), LANES)
+                src = srcs.at[pl.ds(nz * tc, nz), pl.ds(pl.multiple_of(ny * tw, 8), ny), :]
+                dst = dst_ref.at[:, :, pl.ds(x0, LANES)]
+            remote = pltpu.make_async_remote_copy(
+                src_ref=src, dst_ref=dst, send_sem=send.at[k], recv_sem=recv.at[k],
+                device_id=device, device_id_type=MESH)
+            if k:
+                if phase == "start":
+                    remote.start()
                 else:
-                    tc, tw = lax.rem(a + da, 2), lax.rem(w + dw, 2)
-                    device = (4 * h + 2 * c + tc, tw)
-                    x0 = pl.multiple_of(LANES * slab_of(a, w), LANES)
-                    src = srcs[i].at[pl.ds(nz * tc, nz), pl.ds(pl.multiple_of(ny * tw, 8), ny), :]
-                    dst = dsts[i].at[:, :, pl.ds(x0, LANES)]
-                    mine = jnp.logical_and(c == a, jnp.logical_and(tc == c, tw == w))
-                remote = pltpu.make_async_remote_copy(
-                    src_ref=src, dst_ref=dst, send_sem=send.at[i, k], recv_sem=recv.at[i, k],
-                    device_id=device, device_id_type=MESH)
-                if phase == "start":
-                    @pl.when(mine)
-                    def _():
-                        pltpu.make_async_copy(src, dst, local.at[i]).start()
-
-                    @pl.when(jnp.logical_not(mine))
-                    def _():
-                        remote.start()
-                else:
-                    @pl.when(mine)
-                    def _():
-                        pltpu.make_async_copy(src, dst, local.at[i]).wait()
-
-                    @pl.when(jnp.logical_not(mine))
-                    def _():
-                        remote.wait()
-
-
-def spread(arrays, nz, ny, nx, back, cid):
-    n = len(arrays)
-    shape = (nz, ny, nx) if back else (2 * nz, 2 * ny, LANES)
+                    remote.wait()
+                continue
+            here = pltpu.make_async_copy(src, dst, local)
+            if phase == "start":
+                @pl.when(c == a)
+                def _():
+                    here.start()
+
+                @pl.when(c != a)
+                def _():
+                    remote.start()
+            else:
+                @pl.when(c == a)
+                def _():
+                    here.wait()
+
+                @pl.when(c != a)
+                def _():
+                    remote.wait()
+        if phase == "start" and between is not None:
+            between()
+
+
+SPREAD_SEMS = [
+    pltpu.SemaphoreType.DMA((4,)),
+    pltpu.SemaphoreType.DMA((4,)),
+    pltpu.SemaphoreType.DMA,
+]
+
+
+def back_kernel(nz, ny, src, dst, send, recv, local):
+    spread_kernel(nz, ny, True, src, dst, send, recv, local)
+
+
+def gather_back(current, nz, ny, nx):
+    return pl.pallas_call(
+        functools.partial(back_kernel, nz, ny),
+        out_shape=jax.ShapeDtypeStruct((nz, ny, nx), jnp.float32),
+        in_specs=[pl.BlockSpec(memory_space=pl.ANY)],
+        out_specs=pl.BlockSpec(memory_space=pl.ANY),
+        scratch_shapes=SPREAD_SEMS,
+        compiler_params=pltpu.CompilerParams(collective_id=2, has_side_effects=True),
+    )(current)
+
+
+def taps_of(profile, view, radius, reach):
+    kept = []
+    for k in range(2 * reach + 1):
+        value = jnp.full((8, LANES), profile[view, k], jnp.float32)
+        kept.append(jnp.where(abs(k - reach) <= radius, value, jnp.zeros_like(value)))
+    total = kept[0]
+    for value in kept[1:]:
+        total = total + value
+    return [value / total for value in kept]
+
+
+def band(taps, which):
+    total = jnp.zeros(which.shape, jnp.float32)
+    for k, tap in enumerate(taps):
+        total = jnp.where(which == k, tap[0:1, :], total)
+    return split(total)
+
+
+def first_kernel(nz, ny, views, est, psf_z, psf_y, psf_x, extents, order, *refs):
+    n = 2 * views
+    dst, wz, ym, xm, xe = refs[0], refs[1:1 + n], refs[1 + n:1 + 2 * n], refs[1 + 2 * n:1 + 3 * n], refs[1 + 3 * n:1 + 4 * n]
+    send, recv, local = refs[1 + 4 * n:]
+    rows = 2 * ny
+
+    def build():
+        def iota(shape, dim):
+            return lax.broadcasted_iota(jnp.int32, shape, dim)
+
+        y_which = lax.rem(iota((rows, LANES), 1), rows) - iota((rows, LANES), 0) + RL
+        x_which = iota((LANES, LANES), 0) - iota((LANES, LANES), 1) + RL
+        r = iota((16, LANES), 0)
+        e_which = jnp.where(r < 8, r - 8, r + (LANES - 8)) - iota((16, LANES), 1) + RL
+        for p in range(views):
+            view = order[p]
+            tz = taps_of(psf_z, view, (extents[view, 0] - 1) // 2, RZ)
+            ty = taps_of(psf_y, view, (extents[view, 1] - 1) // 2, RL)
+            tx = taps_of(psf_x, view, (extents[view, 2] - 1) // 2, RL)
+            for i in (2 * p, 2 * p + 1):
+                for k in range(2 * RZ + 1):
+                    wz[i][k] = tz[k]
+                hi, lo = band(ty, y_which)
+                ym[i][:, :LANES] = hi
+                ym[i][:, LANES:] = lo
+                hi, lo = band(tx, x_which)
+                for top in (0, LANES):
+                    xm[i][top:top + LANES, :LANES] = hi
+                    xm[i][top:top + LANES, LANES:] = lo
+                hi, lo = band(tx, e_which)
+                xe[i][...] = jnp.zeros_like(xe[i])
+                for top in (0, LANES):
+                    xe[i][top:top + 16, :LANES] = hi
+                    xe[i][top:top + 16, LANES:] = lo
+                tz, ty, tx = tz[::-1], ty[::-1], tx[::-1]
+
+    spread_kernel(nz, ny, False, est, dst, send, recv, local, build)
+
+
+def spread_first(estimate, psf_z, psf_y, psf_x, extents, order):
+    nz, ny, nx = estimate.shape
+    views = order.shape[0]
+    n = 2 * views
+    smem = pl.BlockSpec(memory_space=pltpu.SMEM)
+    vmem = pl.BlockSpec(memory_space=pltpu.VMEM)
+    like = jax.ShapeDtypeStruct
     out = pl.pallas_call(
-        functools.partial(spread_kernel, nz, ny, back, n),
-        out_shape=[jax.ShapeDtypeStruct(shape, jnp.float32)] * n,
-        in_specs=[pl.BlockSpec(memory_space=pl.ANY)] * n,
-        out_specs=[pl.BlockSpec(memory_space=pl.ANY)] * n,
-        scratch_shapes=[
-            pltpu.SemaphoreType.DMA((n, 4)),
-            pltpu.SemaphoreType.DMA((n, 4)),
-            pltpu.SemaphoreType.DMA((n,)),
-        ],
-        compiler_params=pltpu.CompilerParams(collective_id=cid, has_side_effects=True),
-    )(*arrays)
-    return out
+        functools.partial(first_kernel, nz, ny, views),
+        out_shape=[like((2 * nz, 2 * ny, LANES), jnp.float32)]
+        + [like((2 * RZ + 1, 8, LANES), jnp.float32)] * n
+        + [like((2 * ny, 2 * LANES), jnp.bfloat16)] * n
+        + [like((2 * LANES, 2 * LANES), jnp.bfloat16)] * (2 * n),
+        in_specs=[pl.BlockSpec(memory_space=pl.ANY)] + [smem] * 5,
+        out_specs=[pl.BlockSpec(memory_space=pl.ANY)] + [vmem] * (4 * n),
+        scratch_shapes=SPREAD_SEMS,
+        compiler_params=pltpu.CompilerParams(collective_id=1, has_side_effects=True),
+    )(estimate, psf_z, psf_y, psf_x, extents, order)
+    return out[0], [out[1 + i::n][:4] for i in range(n)]
 
 
 def split(value):
@@ -159,8 +245,26 @@
 CHUNKS = 4
 
 
-def blur_kernel(divide, chain, f, other, wz, ym, xm, xe, out,
-                below, above, zb, pack_l, pack_r, got_l, got_r, zs, zr, xs, xr):
+def blur_kernel(kind, chain, *refs):
+    divide = kind in (0, 2)
+    refs = list(refs)
+    f = refs.pop(0)
+    other = refs.pop(0) if kind else None
+    wz, ym, xm, xe = [refs.pop(0) for _ in range(4)]
+    if kind < 3:
+        view, measured = refs.pop(0), refs.pop(0)
+    out = refs.pop(0)
+    if kind == 1:
+        moved = refs.pop(0)
+    below, above, zb, pack_l, pack_r, got_l, got_r, zs, zr, xs, xr = refs[:11]
+    refs = refs[11:]
+    if kind < 3:
+        stage, chosen, bs, br, bl = refs[:5]
+        if kind != 1:
+            moved = refs[5]
+        nb = chosen.shape[0]
+        ny = chosen.shape[1]
+        nz = measured.shape[1]
     planes, rows, _ = f.shape
     h, a, c, w = place()
     zi = 2 * h + c
@@ -179,11 +283,25 @@
     lf, rt = x_dev(lax.rem(s + 3, 4)), x_dev(lax.rem(s + 1, 4))
 
     barrier = pltpu.get_barrier_semaphore()
-    for there, device in ((has_up, up), (has_dn, dn), (has_l, lf), (has_r, rt)):
+    greet = [(has_up, up), (has_dn, dn), (has_l, lf), (has_r, rt)]
+    for there, device in greet:
         @pl.when(there)
         def _():
             pl.semaphore_signal(barrier, inc=1, device_id=device, device_id_type=MESH)
-    peers = sum(there.astype(jnp.int32) for there in (has_up, has_dn, has_l, has_r))
+    peers = sum(there.astype(jnp.int32) for there, _ in greet)
+    if kind < 3:
+        for k in range(4):
+            device = (4 * h + 2 * c + lax.rem(a + k // 2, 2), lax.rem(w + k % 2, 2))
+            if k:
+                pl.semaphore_signal(barrier, inc=1, device_id=device, device_id_type=MESH)
+            else:
+                @pl.when(c != a)
+                def _():
+                    pl.semaphore_signal(barrier, inc=1, device_id=device, device_id_type=MESH)
+        peers = peers + 3 + (c != a).astype(jnp.int32)
+        start = nz // 2 if kind == 2 else 0
+        fetch = pltpu.make_async_copy(measured.at[:, pl.ds(start, nb)], stage, bl)
+        fetch.start()
     pl.semaphore_wait(barrier, peers)
 
     part = rows // CHUNKS
@@ -215,6 +333,41 @@
         @pl.when(has_dn)
         def _():
             z_copy(1, j).start()
+
+    def bulk(k):
+        da, dw = k // 2, k % 2
+        ta, tw = lax.rem(c + da, 2), lax.rem(w + dw, 2)
+        x0 = pl.multiple_of(LANES * slab_of(ta, tw), LANES)
+        return pltpu.make_async_remote_copy(
+            src_ref=chosen.at[:, :, pl.ds(x0, LANES)],
+            dst_ref=moved.at[pl.ds(nb * c, nb), pl.ds(pl.multiple_of(ny * w, 8), ny), :],
+            send_sem=bs.at[k], recv_sem=br.at[k],
+            device_id=(4 * h + 2 * ta + a, tw), device_id_type=MESH)
+
+    def bulk_wait():
+        for k in range(4):
+            if k:
+                bulk(k).wait()
+            else:
+                @pl.when(c != a)
+                def _():
+                    bulk(0).wait()
+
+    if kind < 3:
+        fetch.wait()
+        chosen[...] = stage[view[0]]
+
+        @pl.when(c != a)
+        def _():
+            bulk(0).start()
+
+        for k in range(1, 4):
+            bulk(k).start()
+
+        @pl.when(c == a)
+        def _():
+            x0 = pl.multiple_of(LANES * slab_of(c, w), LANES)
+            moved[pl.ds(nb * c, nb), pl.ds(pl.multiple_of(ny * w, 8), ny), :] = chosen[:, :, pl.ds(x0, LANES)]
 
     @pl.when(jnp.logical_not(has_dn))
     def _():
@@ -323,6 +476,9 @@
     def _():
         x_copy(1).wait_recv()
 
+    if divide:
+        bulk_wait()
+
     for p in range(0, planes, step):
         edges = []
         for i in range(step):
@@ -335,8 +491,13 @@
         hi, lo = split(jnp.concatenate(edges, axis=0))
         got = jnp.dot(jnp.concatenate([hi, lo], axis=1), xe[...], preferred_element_type=jnp.float32)
         value = zb[p:p + step] + (got[:, :LANES] + got[:, LANES:]).reshape(step, rows, LANES)
-        if divide:
-            out[p:p + step] = other[p:p + step] / value
+        if kind == 0:
+            out[p:p + step] = moved[p:p + step] / value
+        elif kind == 2:
+            block, within = divmod(p, nz)
+            held = other if within < nb else moved
+            at = block * nb + within % nb
+            out[p:p + step] = held[at:at + step] / value
         else:
             out[p:p + step] = other[p:p + step] * value
 
@@ -348,77 +509,68 @@
     def _():
         x_copy(1).wait_send()
 
-
-def slab_blur(f, other, wz, ym, xm, xe, divide, chain):
+    if kind == 1:
+        bulk_wait()
+
+
+def slab_blur(kind, chain, f, other, weights, view, measured):
     planes, rows, _ = f.shape
     vmem = pl.BlockSpec(memory_space=pltpu.VMEM)
     packs = pltpu.VMEM((planes * 8 // LANES, rows, LANES), jnp.float32)
-    return pl.pallas_call(
-        functools.partial(blur_kernel, divide, chain),
-        out_shape=jax.ShapeDtypeStruct(f.shape, jnp.float32),
-        in_specs=[vmem] * 6,
-        out_specs=vmem,
-        scratch_shapes=[
-            pltpu.VMEM((RZ, rows, LANES), jnp.float32),
-            pltpu.VMEM((RZ, rows, LANES), jnp.float32),
-            pltpu.VMEM((planes, rows, LANES), jnp.float32),
-            packs, packs, packs, packs,
-            pltpu.SemaphoreType.DMA((2, CHUNKS)),
-            pltpu.SemaphoreType.DMA((2, CHUNKS)),
-            pltpu.SemaphoreType.DMA((2,)),
-            pltpu.SemaphoreType.DMA((2,)),
-        ],
-        compiler_params=pltpu.CompilerParams(
-            collective_id=3 if divide else 4, has_side_effects=True),
-    )(f, other, wz, ym, xm, xe)
-
-
-def halves(value):
-    hi = lax.reduce_precision(value, 8, 7)
-    return hi.astype(jnp.bfloat16), (value - hi).astype(jnp.bfloat16)
-
-
-def band(weights, source, target, reach):
-    which = source[:, None] - target[None, :] + reach
-    total = jnp.zeros((weights.shape[0],) + which.shape, jnp.float32)
-    for k in range(2 * reach + 1):
-        total = jnp.where(which == k, weights[:, k][:, None, None], total)
-    return total
-
-
-def all_taps(profiles, radii, reach):
-    offsets = jnp.abs(jnp.arange(2 * reach + 1, dtype=jnp.int32) - reach)
-    kept = jnp.where(offsets[None] <= radii[:, None], profiles, 0.0)
-    taps = kept / jnp.sum(kept, axis=1, keepdims=True)
-    return jnp.stack([taps, taps[:, ::-1]], axis=1).reshape(-1, 2 * reach + 1)
+    like = jax.ShapeDtypeStruct
+    args = [f] + ([other] if kind else []) + list(weights)
+    in_specs = [vmem] * len(args)
+    out_shape = [like(f.shape, jnp.float32)]
+    scratch = [
+        pltpu.VMEM((RZ, rows, LANES), jnp.float32),
+        pltpu.VMEM((RZ, rows, LANES), jnp.float32),
+        pltpu.VMEM((planes, rows, LANES), jnp.float32),
+        packs, packs, packs, packs,
+        pltpu.SemaphoreType.DMA((2, CHUNKS)),
+        pltpu.SemaphoreType.DMA((2, CHUNKS)),
+        pltpu.SemaphoreType.DMA((2,)),
+        pltpu.SemaphoreType.DMA((2,)),
+    ]
+    if kind < 3:
+        views, nz, ny, nx = measured.shape
+        nb = nz if kind == 0 else nz // 2
+        args += [view, measured]
+        in_specs += [pl.BlockSpec(memory_space=pltpu.SMEM), pl.BlockSpec(memory_space=pl.ANY)]
+        scratch += [
+            pltpu.VMEM((views, nb, ny, nx), jnp.float32),
+            pltpu.VMEM((nb, ny, nx), jnp.float32),
+            pltpu.SemaphoreType.DMA((4,)),
+            pltpu.SemaphoreType.DMA((4,)),
+            pltpu.SemaphoreType.DMA,
+        ]
+        if kind == 1:
+            out_shape.append(like((2 * nb, rows, LANES), jnp.float32))
+        else:
+            scratch.append(pltpu.VMEM((2 * nb, rows, LANES), jnp.float32))
+    out = pl.pallas_call(
+        functools.partial(blur_kernel, kind, chain),
+        out_shape=out_shape,
+        in_specs=in_specs,
+        out_specs=[vmem] * len(out_shape),
+        scratch_shapes=scratch,
+        compiler_params=pltpu.CompilerParams(collective_id=3 + kind, has_side_effects=True),
+    )(*args)
+    return out
 
 
 def slabs(chain, estimate, measured, psf_z, psf_y, psf_x, extents, order):
     views, nz, ny, nx = measured.shape
-    rows = 2 * ny
-    radii = ((extents - 1) // 2)[order]
-    wz = all_taps(psf_z[order], radii[:, 0], RZ)
-    wy = all_taps(psf_y[order], radii[:, 1], RL)
-    wx = all_taps(psf_x[order], radii[:, 2], RL)
-    wz = jnp.broadcast_to(wz[:, :, None, None], wz.shape + (8, LANES))
-    cells = jnp.arange(rows, dtype=jnp.int32)
-    hi, lo = halves(band(wy, cells, cells, RL).swapaxes(1, 2))
-    ym = jnp.concatenate([hi, hi, lo, lo], axis=2)
-    cells = jnp.arange(LANES, dtype=jnp.int32)
-    hi, lo = halves(band(wx, cells, cells, RL))
-    xm = jnp.concatenate([jnp.concatenate([hi, lo], axis=2)] * 2, axis=1)
-    edge = jnp.where(cells < 8, cells - 8, jnp.where(cells < 16, LANES - 8 + cells, -4 * LANES))
-    hi, lo = halves(band(wx, edge, cells, RL))
-    xe = jnp.concatenate([jnp.concatenate([hi, lo], axis=2)] * 2, axis=1)
-    recorded = [lax.dynamic_index_in_dim(measured, order[p], 0, keepdims=False) for p in range(views)]
-    moved = spread([estimate] + recorded, nz, ny, nx, False, 1)
-    current = moved[0]
+    current, weights = spread_first(estimate, psf_z, psf_y, psf_x, extents, order)
+    seen = [order[p:p + 1] for p in range(views)]
+    half = None
     for p in range(views):
-        i = 2 * p
-        ratio = slab_blur(current, moved[1 + p], wz[i], ym[i], xm[i], xe[i], True, chain)
-        i = i + 1
-        current = slab_blur(ratio, current, wz[i], ym[i], xm[i], xe[i], False, chain)
-    return spread([current], nz, ny, nx, True, 2)[0]
+        kind = 2 if p else 0
+        ratio, = slab_blur(kind, chain, current, half, weights[2 * p], seen[p], measured)
+        if p < views - 1:
+            current, half = slab_blur(1, chain, ratio, current, weights[2 * p + 1], seen[p + 1], measured)
+        else:
+            current, = slab_blur(3, chain, ratio, current, weights[2 * p + 1], None, None)
+    return gather_back(current, nz, ny, nx)
 
 
 def on_device(estimate, measured, psf_z, psf_y, psf_x, extents, order):

time: 247 us -> 182 us (0.74)
  Pallas kernels: 208 us -> 176 us
  local copies, waits for them, and re-layouts: 20.5 us -> 3.76 us
  between operations: 7.96 us -> 0.08 us
  other arithmetic: 6.79 us -> 0 us
    pallas_call x10, Pallas kernels: 208 us -> 176 us  [the longest x8 142 us: slab_blur(): pl.pallas_call(functools.partial(blur_kernel, kind, chain), out_shape=out...]
    squeeze x4 -> x0, local copies, waits for them, and re-layouts: 7.15 us -> none  [the longest x1 4.49 us: slabs(): lax.dynamic_index_in_dim(measured, order[p], 0, keepdims=False)]
    broadcast_in_dim x9 -> x0, local copies, waits for them, and re-layouts: 5.99 us -> none  [slabs(): wz = jnp.broadcast_to(wz[:, :, None, None], wz.shape + (8, LANES))]
    convert_element_type x6 -> x0, other arithmetic: 5.07 us -> none  [halves(): return (hi.astype(jnp.bfloat16), (value - hi).astype(jnp.bfloat16))]
where the time goes in v2:
time: 182 us; the launch traced here: 180 us
  Pallas kernels  176 us (97%)
  local copies, waits for them, and re-layouts  3.76 us (2%)
    pallas_call x8, Pallas kernels, slab_blur(): pl.pallas_call(functools.partial(blur_kernel, kind, chain), out_shape=out...  142 us
    pallas_call x1, Pallas kernels, spread_first(): pl.pallas_call(functools.partial(first_kernel, nz, ny, views), out_shape=...  18.2 us
    pallas_call x1, Pallas kernels, gather_back(): pl.pallas_call(functools.partial(back_kernel, nz, ny), out_shape=jax.Shap...  15.7 us

profile of v2, /device:TPU:20, one launch (start us, length us, event | category | flops | bytes accessed | tf_op | source)
XLA Modules:
  0.0 180.1 jit_solution(11747434298048137640)
XLA Ops:
  0.0 1.5 fusion
  1.5 18.2 %shard_map.73 = (f32[32,64,128]{2,1,0:T(8,128)}, f32[31,8,128]{2,1,0:T(8,128)}, f32[31,8,128]{2,1,0:T(8,128)}, f32[31,8,128]{2,1,0:T(8,128)}, f32[31,8,128]{2,1,...) custom-call(f32[16,32,512]{2,1,0:T(8,128)} %est.1, ...), custom_call_target="tpu_custom_call" | custom-call | tf_op jit(solution)/shard_map/pallas_call | solution.py:225
  19.7 20.8 %shard_map.74.refs_0_ = f32[32,64,128]{2,1,0:T(8,128)} custom-call(f32[32,64,128]{2,1,0:T(8,128)} %get-tuple-element.44.refs_0_.refs_1_, f32[31,8,128]{2,1,0:T(8,128)} %get-tuple-element.45.refs_1_, bf16[64,256]{1,0:T(8,128)(2,1)} %get-tuple-element.46.refs_2_, bf16[256,256]{1,0:T(8,128)(2,1)} %get-tuple-element.47.refs_3_, ...), custom_call_target="tpu_custom_call" | custom-call | tf_op jit(solution)/shard_map/pallas_call | solution.py:550
  40.5 16.8 %shard_map.75 = (f32[32,64,128]{2,1,0:T(8,128)}, f32[16,64,128]{2,1,0:T(8,128)}) custom-call(f32[32,64,128]{2,1,0:T(8,128)} %shard_map.74.refs_0_, f32[32,64,128]{2,1,0:T(8,128)} %get-tuple-element.44.refs_0_.refs_1_, f32[31,8,128]{2,1,0:T(8,128)} %get-tuple-element.49.refs_2_, bf16[64,256]{1,0:T(8,128)(2,1)} %get-tuple-element.50.refs_3_, ...), custom_call_target="tpu_custom_call" | custom-call | tf_op jit(solution)/shard_map/pallas_call | solution.py:550
  57.4 18.5 %shard_map.76.refs_0_ = f32[32,64,128]{2,1,0:T(8,128)} custom-call(f32[32,64,128]{2,1,0:T(8,128)} %get-tuple-element.53.refs_0_.refs_1_, f32[16,64,128]{2,1,0:T(8,128)} %get-tuple-element.54.refs_1_, f32[31,8,128]{2,1,0:T(8,128)} %get-tuple-element.55.refs_2_, bf16[64,256]{1,0:T(8,128)(2,1)} %get-tuple-element.56.refs_3_, ...), custom_call_target="tpu_custom_call" | custom-call | tf_op jit(solution)/shard_map/pallas_call | solution.py:550
  75.9 16.6 %shard_map.77 = (f32[32,64,128]{2,1,0:T(8,128)}, f32[16,64,128]{2,1,0:T(8,128)}) custom-call(f32[32,64,128]{2,1,0:T(8,128)} %shard_map.76.refs_0_, f32[32,64,128]{2,1,0:T(8,128)} %get-tuple-element.53.refs_0_.refs_1_, f32[31,8,128]{2,1,0:T(8,128)} %get-tuple-element.59.refs_2_, bf16[64,256]{1,0:T(8,128)(2,1)} %get-tuple-element.60.refs_3_, ...), custom_call_target="tpu_custom_call" | custom-call | tf_op jit(solution)/shard_map/pallas_call | solution.py:550
  92.5 18.5 %shard_map.78.refs_0_ = f32[32,64,128]{2,1,0:T(8,128)} custom-call(f32[32,64,128]{2,1,0:T(8,128)} %get-tuple-element.63.refs_0_.refs_1_, f32[16,64,128]{2,1,0:T(8,128)} %get-tuple-element.64.refs_1_, f32[31,8,128]{2,1,0:T(8,128)} %get-tuple-element.65.refs_2_, bf16[64,256]{1,0:T(8,128)(2,1)} %get-tuple-element.66.refs_3_, ...), custom_call_target="tpu_custom_call" | custom-call | tf_op jit(solution)/shard_map/pallas_call | solution.py:550
  111.0 16.6 %shard_map.79 = (f32[32,64,128]{2,1,0:T(8,128)}, f32[16,64,128]{2,1,0:T(8,128)}) custom-call(f32[32,64,128]{2,1,0:T(8,128)} %shard_map.78.refs_0_, f32[32,64,128]{2,1,0:T(8,128)} %get-tuple-element.63.refs_0_.refs_1_, f32[31,8,128]{2,1,0:T(8,128)} %get-tuple-element.69.refs_2_, bf16[64,256]{1,0:T(8,128)(2,1)} %get-tuple-element.70.refs_3_, ...), custom_call_target="tpu_custom_call" | custom-call | tf_op jit(solution)/shard_map/pallas_call | solution.py:550
  127.6 18.7 %shard_map.80.refs_0_ = f32[32,64,128]{2,1,0:T(8,128)} custom-call(f32[32,64,128]{2,1,0:T(8,128)} %get-tuple-element.73.refs_0_.refs_1_, f32[16,64,128]{2,1,0:T(8,128)} %get-tuple-element.74.refs_1_, f32[31,8,128]{2,1,0:T(8,128)} %get-tuple-element.75.refs_2_, bf16[64,256]{1,0:T(8,128)(2,1)} %get-tuple-element.76.refs_3_, ...), custom_call_target="tpu_custom_call" | custom-call | tf_op jit(solution)/shard_map/pallas_call | solution.py:550
  146.3 15.8 %shard_map.81.src = f32[32,64,128]{2,1,0:T(8,128)} custom-call(f32[32,64,128]{2,1,0:T(8,128)} %shard_map.80.refs_0_, f32[32,64,128]{2,1,0:T(8,128)} %get-tuple-element.73.refs_0_.refs_1_, f32[31,8,128]{2,1,0:T(8,128)} %get-tuple-element.79.refs_2_, bf16[64,256]{1,0:T(8,128)(2,1)} %get-tuple-element.80.refs_3_, bf16[256,256]{1,0:T(8,128)(2,1)} %get-tuple-element.81.refs_4_, ...), custom_call_target="tpu_custom_call" | custom-call | tf_op jit(solution)/shard_map/pallas_call | solution.py:550
  162.1 15.7 %shard_map.82 = f32[16,32,512]{2,1,0:T(8,128)} custom-call(f32[32,64,128]{2,1,0:T(8,128)} %shard_map.81.src), custom_call_target="tpu_custom_call" | custom-call | tf_op jit(solution)/shard_map/pallas_call | solution.py:151
  177.9 2.3 %copy.9 = f32[16,32,512]{2,1,0:T(8,128)} copy(f32[16,32,512]{2,1,0:T(8,128)} %shard_map.82) | data formatting | bytes 2097152
